TPU v7x, 32 devices: a whole 2x2x4 slice. The times are simulated.
32 devices in a mesh: dp: 2 (over x), etp: 4 (over z), ep: 4 (over y, core).
Axes of the slice: x: 2, y: 2, z: 4, core: 2. Of those that a mesh axis runs over, the one named last changes fastest.
Arguments:
- x_in: bfloat16 [1024, 1536], P(('dp', 'ep')), parts along dimension 0
- y_grad: bfloat16 [1024, 1536], P(('dp', 'ep')), parts along dimension 0
- prim_exp: int32 [1024], P(('dp', 'ep')), parts along dimension 0
- alt_exp: int32 [1024], P(('dp', 'ep')), parts along dimension 0
- w_router: bfloat16 [1536, 40], replicated
- exp_gate: bfloat16 [40, 1536, 512], P('ep', None, 'etp')
- exp_up: bfloat16 [40, 1536, 512], P('ep', None, 'etp')
- exp_down: bfloat16 [40, 512, 1536], P('ep', 'etp')
- sh_gate: bfloat16 [1536, 512], P(None, 'etp')
- sh_up: bfloat16 [1536, 512], P(None, 'etp')
- sh_down: bfloat16 [512, 1536], P('etp')
Outputs:
- output 1: bfloat16 [1024, 1536], P(('dp', 'ep')), parts along dimension 0
- output 2: bfloat16 [1024, 1536], P(('dp', 'ep')), parts along dimension 0
- output 3: float32 [80, 1536, 512], P(('dp', 'ep'), None, 'etp'), parts along dimension 0
- output 4: float32 [80, 1536, 512], P(('dp', 'ep'), None, 'etp'), parts along dimension 0
- output 5: float32 [80, 512, 1536], P(('dp', 'ep'), 'etp'), parts along dimension 0
- output 6: float32 [3072, 512], P('dp', 'etp'), parts along dimension 0
- output 7: float32 [3072, 512], P('dp', 'etp'), parts along dimension 0
- output 8: float32 [1024, 1536], P(('dp', 'etp')), parts along dimension 0
- output 9: float32 [3072, 40], P('dp'), parts along dimension 0
There are 2 independent parts. A program takes and returns all parts, laid end to end along the dimension named above; an argument that names none is the same for every part.
All inputs are finite; a program needn't handle non-finite values.
Results may differ from a plain program's by a relative error of at most 0.00232.
Values are sent between devices in bfloat16 or wider.
A program may use at most 1 GiB of HBM per device.

v0:
```python
import jax
import jax.numpy as jnp
from jax import lax
from jax.sharding import PartitionSpec as P

EPS = 1e-5
F32 = jnp.float32
BF16 = jnp.bfloat16


def exclusive_rank(onehot):
    return jnp.sum((jnp.cumsum(onehot, axis=0) - onehot) * onehot, axis=1)


def glu_grads(d_hidden, act_gate, act_up):
    sig_gate = jax.nn.sigmoid(act_gate)
    d_gate = (d_hidden * act_up * sig_gate * (1.0 + act_gate * (1.0 - sig_gate))).astype(BF16)
    d_up = (d_hidden * act_gate * sig_gate).astype(BF16)
    return d_gate, d_up


def solution(mesh):
    ep_size = mesh.shape["ep"]
    tok_spec = P(("dp", "ep"), None)
    id_spec = P(("dp", "ep"))
    in_specs = (tok_spec, tok_spec, id_spec, id_spec, P(None, None), P("ep", None, "etp"), P("ep", None, "etp"), P("ep", "etp", None), P(None, "etp"), P(None, "etp"), P("etp", None))
    out_specs = (tok_spec, tok_spec, P(("dp", "ep"), None, "etp"), P(("dp", "ep"), None, "etp"), P(("dp", "ep"), "etp", None), P("dp", "etp"), P("dp", "etp"), P(("dp", "etp"), None), P("dp", None))

    def local_step(x_in, y_grad, prim_exp, alt_exp, w_router, exp_gate, exp_up, exp_down, sh_gate, sh_up, sh_down):
        tok_local, model_dim = x_in.shape
        num_exp = w_router.shape[1]
        local_exp = exp_gate.shape[0]
        capacity = 5 * tok_local * ep_size // (4 * num_exp)
        my_rank = lax.axis_index("ep")
        expert_ids = jnp.arange(num_exp)
        earlier = (jnp.arange(ep_size) < my_rank).astype(jnp.int32)[:, None]
        x_wide = x_in.astype(F32)
        inv_rms = lax.rsqrt(jnp.mean(x_wide * x_wide, axis=1, keepdims=True) + EPS)
        normed = (x_wide * inv_rms).astype(BF16)
        gate_probs = jax.nn.softmax(jnp.dot(normed, w_router, preferred_element_type=F32), axis=1)
        one_prim = (prim_exp[:, None] == expert_ids[None, :]).astype(jnp.int32)
        prim_counts = lax.all_gather(jnp.sum(one_prim, axis=0), "ep")
        rank_prim = exclusive_rank(one_prim) + jnp.sum(one_prim * jnp.sum(prim_counts * earlier, axis=0)[None, :], axis=1)
        keep_prim = rank_prim < capacity
        kept_count = jnp.minimum(jnp.sum(prim_counts, axis=0), capacity)
        overflow = jnp.logical_not(keep_prim).astype(jnp.int32)
        one_alt = (alt_exp[:, None] == expert_ids[None, :]).astype(jnp.int32) * overflow[:, None]
        alt_counts = lax.all_gather(jnp.sum(one_alt, axis=0), "ep")
        alt_base = kept_count + jnp.sum(alt_counts * earlier, axis=0)
        slot_alt = exclusive_rank(one_alt) + jnp.sum(one_alt * alt_base[None, :], axis=1)
        keep_alt = (overflow == 1) & (slot_alt < capacity)
        assign = jnp.where(keep_prim, prim_exp, jnp.where(keep_alt, alt_exp, -1))
        slot_idx = jnp.where(keep_prim, rank_prim, slot_alt)
        owner_rank = jnp.where(assign >= 0, assign // local_exp, -1)
        to_owner = (owner_rank[None, :] == jnp.arange(ep_size)[:, None])[:, :, None]
        total_rows = ep_size * tok_local
        all_assign = lax.all_gather(assign, "ep", tiled=True)
        all_slot = lax.all_gather(slot_idx, "ep", tiled=True)
        mine_rows = (all_assign >= 0) & (all_assign // local_exp == my_rank)
        target = jnp.where(mine_rows, (all_assign - my_rank * local_exp) * capacity + all_slot, local_exp * capacity)
        slot_table = jnp.full((local_exp * capacity + 1,), total_rows, jnp.int32).at[target].set(jnp.arange(total_rows, dtype=jnp.int32))[: local_exp * capacity]

        def send_out(tok_rows):
            sent_rows = jnp.where(to_owner, tok_rows[None], 0)
            recv_rows = lax.all_to_all(sent_rows, "ep", 0, 0, tiled=True).reshape(total_rows, model_dim)
            return jnp.take(recv_rows, slot_table, axis=0, mode="fill", fill_value=0).reshape(local_exp, capacity, model_dim)

        def send_back(slot_rows):
            flat_rows = jnp.take(slot_rows.reshape(local_exp * capacity, model_dim), target, axis=0, mode="fill", fill_value=0)
            back_rows = lax.all_to_all(flat_rows.reshape(ep_size, tok_local, model_dim), "ep", 0, 0, tiled=True)
            return jnp.sum(back_rows, axis=0).astype(F32)

        expert_rows = send_out(normed)
        act_gate = jnp.einsum("ecd,edf->ecf", expert_rows, exp_gate, preferred_element_type=F32)
        act_up = jnp.einsum("ecd,edf->ecf", expert_rows, exp_up, preferred_element_type=F32)
        hidden = (jax.nn.silu(act_gate) * act_up).astype(BF16)
        out_rows = lax.psum(jnp.einsum("ecf,efd->ecd", hidden, exp_down, preferred_element_type=F32), "etp").astype(BF16)
        tok_out = send_back(out_rows)
        one_assign = (assign[:, None] == expert_ids[None, :]).astype(F32)
        gate_val = jnp.sum(gate_probs * one_assign, axis=1, keepdims=True)
        sh_act_gate = jnp.dot(normed, sh_gate, preferred_element_type=F32)
        sh_act_up = jnp.dot(normed, sh_up, preferred_element_type=F32)
        sh_hidden = (jax.nn.silu(sh_act_gate) * sh_act_up).astype(BF16)
        sh_out = lax.psum(jnp.dot(sh_hidden, sh_down, preferred_element_type=F32), "etp")
        y_out = (x_wide + sh_out + gate_val * tok_out).astype(BF16)
        dy_wide = y_grad.astype(F32)
        d_route = (gate_val * dy_wide).astype(BF16)
        d_rows = send_out(d_route)
        d_hidden = jnp.einsum("ecd,efd->ecf", d_rows, exp_down, preferred_element_type=F32)
        g_exp_down = jnp.einsum("ecf,ecd->efd", hidden, d_rows, preferred_element_type=F32)
        d_gate, d_up = glu_grads(d_hidden, act_gate, act_up)
        g_exp_gate = jnp.einsum("ecd,ecf->edf", expert_rows, d_gate, preferred_element_type=F32)
        g_exp_up = jnp.einsum("ecd,ecf->edf", expert_rows, d_up, preferred_element_type=F32)
        d_rows_in = lax.psum(jnp.einsum("ecf,edf->ecd", d_gate, exp_gate, preferred_element_type=F32) + jnp.einsum("ecf,edf->ecd", d_up, exp_up, preferred_element_type=F32), "etp").astype(BF16)
        dn_routed = send_back(d_rows_in)
        d_gate_val = jnp.sum(dy_wide * tok_out, axis=1, keepdims=True)
        d_logits = (d_gate_val * gate_val * (one_assign - gate_probs)).astype(BF16)
        g_router = lax.psum(jnp.einsum("td,te->de", normed, d_logits, preferred_element_type=F32), "ep")
        dn_router = jnp.einsum("te,de->td", d_logits, w_router, preferred_element_type=F32)
        sh_d_hidden = jnp.einsum("td,fd->tf", y_grad, sh_down, preferred_element_type=F32)
        g_sh_down = lax.psum(jnp.einsum("tf,td->fd", sh_hidden, y_grad, preferred_element_type=F32), "ep")
        sh_d_gate, sh_d_up = glu_grads(sh_d_hidden, sh_act_gate, sh_act_up)
        g_sh_gate = lax.psum(jnp.einsum("td,tf->df", normed, sh_d_gate, preferred_element_type=F32), "ep")
        g_sh_up = lax.psum(jnp.einsum("td,tf->df", normed, sh_d_up, preferred_element_type=F32), "ep")
        dn_shared = lax.psum(jnp.einsum("tf,df->td", sh_d_gate, sh_gate, preferred_element_type=F32) + jnp.einsum("tf,df->td", sh_d_up, sh_up, preferred_element_type=F32), "etp")
        d_normed = dn_shared + dn_router + dn_routed
        norm_proj = jnp.mean(d_normed * x_wide, axis=1, keepdims=True)
        x_grad = (dy_wide + inv_rms * d_normed - x_wide * inv_rms ** 3 * norm_proj).astype(BF16)
        return (y_out, x_grad, g_exp_gate, g_exp_up, g_exp_down, g_sh_gate, g_sh_up, g_sh_down, g_router)

    return jax.shard_map(local_step, mesh=mesh, in_specs=in_specs, out_specs=out_specs, check_vma=False)
```

profile of v0, /device:TPU:0, one launch (start us, length us, event | category | flops | bytes accessed | tf_op | source)
XLA Modules:
  0.0 296.1 jit_solution(7934267927196813484)
XLA Ops:
  8.8 1.2 fusion.7
  10.0 1.2 dynamic-slice
  12.1 6.4 %all-reduce = s32[160]{0:T(256)S(1)} all-reduce(s32[160]{0:T(256)S(1)} %dynamic-update-slice), channel_id=2, replica_groups=mesh['dp'=2,'etp'=4,'ep'=4] {'ep'}, use_global_device_ids=true, to_apply=%add | all-reduce | flops 160 | bytes 1280
  20.8 4.3 %all-reduce.1 = s32[160]{0:T(256)S(1)} all-reduce(s32[160]{0:T(256)S(1)} %dynamic-update-slice.1), channel_id=3, replica_groups=mesh['dp'=2,'etp'=4,'ep'=4] {'ep'}, use_global_device_ids=true, to_apply=%add.1 | all-reduce | flops 160 | bytes 1280
  25.4 0.8 multiply_reduce_fusion
  27.0 1.1 fusion.8
  28.6 2.0 broadcast_select_fusion.2
  30.6 3.7 %all-to-all-start.2 = ((bf16[4,128,1536]{2,1,0:T(8,128)(2,1)}), bf16[4,128,1536]{2,1,0:T(8,128)(2,1)S(1)}, u32[]{:S(2)}, u32[]{:S(2)}) async-start(bf16[4,128,1536]{2,1,0:T(8,128)(2,1)} %get-tuple-element.54), calls=%async_computation.2 | async-start | bytes 3145728 | tf_op jit(solution)/shard_map/all_to_all | solution.py:65
  34.3 1.2 fusion.29
  36.4 1.1 fusion.30
  37.5 1.1 convolution_add_fusion.2
  38.7 16.2 %all-gather.2 = s32[4,1,128]{2,1,0:T(1,128)S(1)} all-gather(s32[1,1,128]{2,1,0:T(1,128)S(1)} %bitcast.72), channel_id=1, replica_groups=mesh['dp'=2,'etp'=4,'ep'=4] {'ep'}, dimensions={0}, use_global_device_ids=true | all-gather | bytes 2560 | tf_op jit(solution)/shard_map/all_gather | solution.py:57
  54.9 5.1 %all-gather.3 = s32[4,1,128]{2,1,0:T(1,128)S(1)} all-gather(s32[1,1,128]{2,1,0:T(1,128)S(1)} %get-tuple-element.45), channel_id=1, replica_groups=mesh['dp'=2,'etp'=4,'ep'=4] {'ep'}, dimensions={0}, use_global_device_ids=true | all-gather | bytes 2560 | tf_op jit(solution)/shard_map/all_gather | solution.py:58
  60.0 4.3 %all-to-all-start = ((bf16[4,128,1536]{2,1,0:T(8,128)(2,1)}), bf16[4,128,1536]{2,1,0:T(8,128)(2,1)}, u32[]{:S(2)}, u32[]{:S(2)}) async-start(bf16[4,128,1536]{2,1,0:T(8,128)(2,1)} %get-tuple-element.55), calls=%async_computation | async-start | bytes 3145728 | tf_op jit(solution)/shard_map/all_to_all | solution.py:65
  64.4 2.4 scatter_custom_fusion
  66.9 1.0 gather_fusion.2
  67.9 16.2 %all-to-all-done = bf16[4,128,1536]{2,1,0:T(8,128)(2,1)} async-done(((bf16[4,128,1536]{2,1,0:T(8,128)(2,1)}), bf16[4,128,1536]{2,1,0:T(8,128)(2,1)}, u32[]{:S(2)}, u32[]{:S(2)}) %all-to-all-start) | async-done | bytes 1572896 | tf_op jit(solution)/shard_map/all_to_all | solution.py:65
  84.2 3.1 %gather_fusion = bf16[160,1536]{1,0:T(8,128)(2,1)S(1)} fusion(bf16[512,1536]{1,0:T(8,128)(2,1)} %bitcast.5, s32[1024]{0:T(1024)S(1)} %pad_clamp_fusion.1), kind=kCustom, calls=%fused_computation.clone | custom fusion | bytes 983680 | tf_op jit(solution)/shard_map/jit(_take)/gather | solution.py:66
  87.4 3.0 fusion.32
  91.5 1.5 copy-done.4
  93.0 1.1 multiply_convert_fusion
  94.1 1.1 fusion.35
  95.2 1.0 copy-done.3
  96.2 2.1 convolution_add_fusion
  98.3 1.6 fusion.33
  99.9 74.7 %all-reduce.12 = (bf16[10,16,1536]{2,1,0:T(8,128)(2,1)S(1)}, bf16[10,16,1536]{2,1,0:T(8,128)(2,1)S(1)}) all-reduce(f32[10,16,1536]{2,1,0:T(8,128)} %fusion.33, f32[10,16,1536]{2,1,0:T(8,128)} %convolution_add_fusion), channel_id=1, replica_groups=mesh['dp'=2,'etp'=4,'ep'=4] {'etp'}, use_global_device_ids=true, to_apply=%region_17.19 | all-reduce | flops 491520 | bytes 2949120 | tf_op jit(solution)/shard_map/psum | solution.py:77
  174.6 2.9 gather_fusion.3
  177.6 2.9 gather_fusion.1
  180.5 3.8 %broadcast_select_fusion = (bf16[512,1536]{1,0:T(8,128)(2,1)}, bf16[512,1536]{1,0:T(8,128)(2,1)}) fusion(bf16[512,1536]{1,0:T(8,128)(2,1)} %gather_fusion.3, pred[512]{0:T(512)(128)(4,1)S(1)} %get-tuple-element.27, bf16[512,1536]{1,0:T(8,128)(2,1)} %gather_fusion.1), kind=kLoop, calls=%fused_computation.14 | loop fusion | flops 1572864 | bytes 6291968 | tf_op jit(solution)/shard_map/jit(_take)/select_n | solution.py:69
  184.3 3.6 %all-to-all-start.1 = ((bf16[4,128,1536]{2,1,0:T(8,128)(2,1)}), bf16[4,128,1536]{2,1,0:T(8,128)(2,1)S(1)}, u32[]{:S(2)}, u32[]{:S(2)}) async-start(bf16[4,128,1536]{2,1,0:T(8,128)(2,1)} %bitcast.69), calls=%async_computation.1 | async-start | bytes 3145728 | tf_op jit(solution)/shard_map/all_to_all | solution.py:70
  187.9 1.2 fusion.40
  189.1 1.2 fusion.39
  190.3 1.2 fusion.41
  191.5 4.4 %fusion.38 = f32[10,128,1536]{2,1,0:T(8,128)} fusion(bf16[10,16,128]{2,1,0:T(8,128)(2,1)S(1)} %get-tuple-element.37, bf16[10,16,1536]{2,1,0:T(8,128)(2,1)S(1)} %bitcast.71), kind=kOutput, calls=%fused_computation.104 | convolution fusion | flops 62914560 | bytes 8396800 | tf_op jit(solution)/shard_map/ecf,ecd->efd/dot_general | solution.py:90
  195.9 11.7 %all-to-all-done.1 = bf16[4,128,1536]{2,1,0:T(8,128)(2,1)S(1)} async-done(((bf16[4,128,1536]{2,1,0:T(8,128)(2,1)}), bf16[4,128,1536]{2,1,0:T(8,128)(2,1)S(1)}, u32[]{:S(2)}, u32[]{:S(2)}) %all-to-all-start.1) | async-done | bytes 1572896 | tf_op jit(solution)/shard_map/all_to_all | solution.py:70
  207.7 1.1 copy-done.5
  208.8 3.6 %all-to-all-start.3 = ((bf16[4,128,1536]{2,1,0:T(8,128)(2,1)}), bf16[4,128,1536]{2,1,0:T(8,128)(2,1)S(1)}, u32[]{:S(2)}, u32[]{:S(2)}) async-start(bf16[4,128,1536]{2,1,0:T(8,128)(2,1)} %bitcast.68), calls=%async_computation.3 | async-start | bytes 3145728 | tf_op jit(solution)/shard_map/all_to_all | solution.py:70
  212.4 4.5 %fusion.37 = f32[10,1536,128]{2,1,0:T(8,128)} fusion(bf16[10,16,1536]{2,1,0:T(8,128)(2,1)S(1)} %bitcast.66, bf16[10,16,128]{2,1,0:T(8,128)(2,1)S(1)} %get-tuple-element.35), kind=kOutput, calls=%fused_computation.103 | convolution fusion | flops 62914560 | bytes 8396800 | tf_op jit(solution)/shard_map/ecd,ecf->edf/dot_general | solution.py:93
  217.0 1.7 reduce_sum.162
  218.9 0.9 fusion.24
  219.8 4.5 %fusion.36 = f32[10,1536,128]{2,1,0:T(8,128)} fusion(bf16[10,16,1536]{2,1,0:T(8,128)(2,1)S(1)} %bitcast.67, bf16[10,16,128]{2,1,0:T(8,128)(2,1)S(1)} %get-tuple-element.36), kind=kOutput, calls=%fused_computation.102 | convolution fusion | flops 62914560 | bytes 8396800 | tf_op jit(solution)/shard_map/ecd,ecf->edf/dot_general | solution.py:92
  224.3 11.7 %all-to-all-done.3 = bf16[4,128,1536]{2,1,0:T(8,128)(2,1)S(1)} async-done(((bf16[4,128,1536]{2,1,0:T(8,128)(2,1)}), bf16[4,128,1536]{2,1,0:T(8,128)(2,1)S(1)}, u32[]{:S(2)}, u32[]{:S(2)}) %all-to-all-start.3) | async-done | bytes 1572896 | tf_op jit(solution)/shard_map/all_to_all | solution.py:70
  236.3 1.6 fusion.10
  238.0 1.3 fusion.6
  239.3 45.4 %all-reduce.9.cloned.1.call-done = (f32[1536,128]{1,0:T(8,128)}, f32[1536,128]{1,0:T(8,128)}, f32[128,1536]{1,0:T(8,128)}, f32[1536,40]{0,1:T(8,128)}) async-done(((f32[1536,128]{1,0:T(8,128)}, f32[1536,128]{1,0:T(8,128)}, f32[128,1536]{1,0:T(8,128)}, f32[1536,40]{0,1:T(8,128)}), (f32[1536,128]{1,0:T(8,128)}, f32[1536,128]{1,0:T(8,128)}, f32[128,1536]{1,0:T(8,128)}, ...) | async-done | bytes 2605072 | tf_op jit(solution)/shard_map/psum | solution.py:103
  284.6 2.2 copy.34
  286.8 0.9 copy.35
  287.7 0.9 copy.36
  (80 shorter events, 9.0 us)
Async XLA Ops:
  7.2 28.7 %copy-start = (bf16[128,1536]{1,0:T(8,128)(2,1)S(1)}, bf16[128,1536]{1,0:T(8,128)(2,1)}, u32[]{:S(2)}) copy-start(bf16[128,1536]{1,0:T(8,128)(2,1)} %param.25) | copy-start | bytes 1179652
  7.2 20.9 %copy-start.15 = (bf16[1536,40]{0,1:T(8,128)(2,1)S(1)}, bf16[1536,40]{0,1:T(8,128)(2,1)}, u32[]{:S(2)}) copy-start(bf16[1536,40]{0,1:T(8,128)(2,1)} %param.19) | copy-start | bytes 368644
  7.2 21.2 %copy-start.7 = (bf16[128,1536]{1,0:T(8,128)(2,1)S(1)}, bf16[128,1536]{1,0:T(8,128)(2,1)}, u32[]{:S(2)}) copy-start(bf16[128,1536]{1,0:T(8,128)(2,1)} %param.16) | copy-start | bytes 1179652
  30.6 5.0 %copy-start.10 = (bf16[1536,128]{1,0:T(8,128)(2,1)S(1)}, bf16[1536,128]{1,0:T(8,128)(2,1)}, u32[]{:S(2)}) copy-start(bf16[1536,128]{1,0:T(8,128)(2,1)} %param.23) | copy-start | bytes 1179652
  30.6 29.4 %all-to-all-start.2 = ((bf16[4,128,1536]{2,1,0:T(8,128)(2,1)}), bf16[4,128,1536]{2,1,0:T(8,128)(2,1)S(1)}, u32[]{:S(2)}, u32[]{:S(2)}) async-start(bf16[4,128,1536]{2,1,0:T(8,128)(2,1)} %get-tuple-element.54), calls=%async_computation.2 | async-start | bytes 3145728 | tf_op jit(solution)/shard_map/all_to_all | solution.py:65
  34.3 202.0 %all-reduce.11.cloned.1.call-start = ((), (), s32[]{:S(2)}) async-start(), calls=%async_computation.5 | async-start | bytes 3145728 | tf_op jit(solution)/shard_map/psum | solution.py:84
  35.9 1.7 copy-start.11
  60.0 24.1 %all-to-all-start = ((bf16[4,128,1536]{2,1,0:T(8,128)(2,1)}), bf16[4,128,1536]{2,1,0:T(8,128)(2,1)}, u32[]{:S(2)}, u32[]{:S(2)}) async-start(bf16[4,128,1536]{2,1,0:T(8,128)(2,1)} %get-tuple-element.55), calls=%async_computation | async-start | bytes 3145728 | tf_op jit(solution)/shard_map/all_to_all | solution.py:65
  87.4 4.1 %copy-start.8 = (bf16[160,1536]{1,0:T(8,128)(2,1)}, bf16[160,1536]{1,0:T(8,128)(2,1)S(1)}, u32[]{:S(2)}) copy-start(bf16[160,1536]{1,0:T(8,128)(2,1)S(1)} %get-tuple-element.52) | copy-start | bytes 1474564
  87.4 3.5 %copy-start.2 = (bf16[10,1536,128]{2,1,0:T(8,128)(2,1)S(1)}, bf16[10,1536,128]{2,1,0:T(8,128)(2,1)}, u32[]{:S(2)}) copy-start(bf16[10,1536,128]{2,1,0:T(8,128)(2,1)} %param.20) | copy-start | bytes 11796484
  90.8 2.1 copy-start.4
  94.1 2.1 copy-start.3
  184.3 23.4 %all-to-all-start.1 = ((bf16[4,128,1536]{2,1,0:T(8,128)(2,1)}), bf16[4,128,1536]{2,1,0:T(8,128)(2,1)S(1)}, u32[]{:S(2)}, u32[]{:S(2)}) async-start(bf16[4,128,1536]{2,1,0:T(8,128)(2,1)} %bitcast.69), calls=%async_computation.1 | async-start | bytes 3145728 | tf_op jit(solution)/shard_map/all_to_all | solution.py:70
  187.9 3.6 %copy-start.9 = (bf16[160,1536]{1,0:T(8,128)(2,1)S(1)}, bf16[160,1536]{1,0:T(8,128)(2,1)}, u32[]{:S(2)}) copy-start(bf16[160,1536]{1,0:T(8,128)(2,1)} %copy-done.8) | copy-start | bytes 1474564
  207.7 1.1 copy-start.5
  208.8 27.2 %all-to-all-start.3 = ((bf16[4,128,1536]{2,1,0:T(8,128)(2,1)}), bf16[4,128,1536]{2,1,0:T(8,128)(2,1)S(1)}, u32[]{:S(2)}, u32[]{:S(2)}) async-start(bf16[4,128,1536]{2,1,0:T(8,128)(2,1)} %bitcast.68), calls=%async_computation.3 | async-start | bytes 3145728 | tf_op jit(solution)/shard_map/all_to_all | solution.py:70
  212.4 72.2 %all-reduce.9.cloned.1.call-start = ((), (), s32[]{:S(2)}) async-start(), calls=%async_computation.4 | async-start | bytes 5210112 | tf_op jit(solution)/shard_map/psum | solution.py:103
  224.3 12.0 %copy-start.6 = (bf16[128,1536]{1,0:T(8,128)(2,1)S(1)}, bf16[128,1536]{1,0:T(8,128)(2,1)}, u32[]{:S(2)}) copy-start(bf16[128,1536]{1,0:T(8,128)(2,1)} %param.15) | copy-start | bytes 1179652
  236.3 1.7 copy-start.14
  284.6 2.2 copy-start.13
  284.6 3.1 %copy-start.12 = (f32[128,1536]{1,0:T(8,128)S(1)}, f32[128,1536]{1,0:T(8,128)}, u32[]{:S(2)}) copy-start(f32[128,1536]{1,0:T(8,128)} %get-tuple-element.67) | copy-start | bytes 2359300
  284.6 4.7 %copy-start.1 = (bf16[128,1536]{1,0:T(8,128)(2,1)S(1)}, bf16[128,1536]{1,0:T(8,128)(2,1)}, u32[]{:S(2)}) copy-start(bf16[128,1536]{1,0:T(8,128)(2,1)} %param.25) | copy-start | bytes 1179652
  286.8 1.8 copy-start.16
Sparse Core Ops, SparseCore 0:
  38.8 73.0 all-reduce.10
  219.9 64.6 all-reduce.8
where the time goes:
time: 297 us; the launch traced here: 296 us
  blocking collectives  107 us (36%)
  waiting for transfers between devices  85.1 us (29%)
  matrix products  33.7 us (11%)
  local copies, waits for them, and re-layouts  23.1 us (8%)
  other arithmetic  17.2 us (6%)
  starting transfers between devices  15.2 us (5%)
  between operations  15.1 us (5%)
    psum x1, blocking collectives, local_step(): lax.psum(jnp.einsum('ecf,efd->ecd', hidden, exp_down, preferred_element_t...  74.7 us
    psum x1, waiting for transfers between devices, local_step(): lax.psum(jnp.einsum('td,tf->df', normed, sh_d_gate, preferred_element_typ...  45.4 us
    all_to_all x2, waiting for transfers between devices, send_back(): lax.all_to_all(flat_rows.reshape(ep_size, tok_local, model_dim), 'ep', 0,...  23.5 us
    all_to_all x2, waiting for transfers between devices, send_out(): lax.all_to_all(sent_rows, 'ep', 0, 0, tiled=True)  16.2 us
    all_gather x1, blocking collectives, local_step(): all_assign = lax.all_gather(assign, 'ep', tiled=True)  16.2 us
    unnamed x2, blocking collectives  10.7 us
    unnamed x43, local copies, waits for them, and re-layouts  10.6 us
    all_to_all x2, starting transfers between devices, send_out(): lax.all_to_all(sent_rows, 'ep', 0, 0, tiled=True)  8.04 us
  transfers between devices with their start and end apart: 6, of which 4 were waited for; matrix products, arithmetic and copies ran while one was open for 18% of the time, Pallas kernels for 0%

commit v1 on v0

v1 whole, which is shorter than its diff:
```python
import functools

import jax
import jax.numpy as jnp
from jax import lax
from jax.experimental import pallas as pl
from jax.experimental.pallas import tpu as pltpu
from jax.sharding import PartitionSpec as P

EPS = 1e-5
F32 = jnp.float32
BF16 = jnp.bfloat16
MESH = pl.DeviceIdType.MESH
TL = 128
NEP = 4
T = TL * NEP
D = 1536
HD = D // 2
E = 40
EL = 10
CAP = 16
W = 128
NM = 18
MR = 32
NC = 4
CR = TL // NC


def dot(a, b):
    return jnp.dot(a, b, preferred_element_type=F32)


def dot_t(a, b):
    return lax.dot_general(a, b, (((1,), (1,)), ((), ())), preferred_element_type=F32)


def tdot(a, b):
    return lax.dot_general(a, b, (((0,), (0,)), ((), ())), preferred_element_type=F32)


def glu(a, b):
    return (a * jax.nn.sigmoid(a) * b).astype(BF16)


def glu_grads(dh, a, b):
    sig = jax.nn.sigmoid(a)
    d_gate = (dh * b * sig * (1.0 + a * (1.0 - sig))).astype(BF16)
    d_up = (dh * a * sig).astype(BF16)
    return d_gate, d_up


def line_kernel(
    x_h, dy_h, prim_v, alt_v, wr_v, wg_h, wu_h, wd_h, sg_h, su_h, sd_h,
    y_o, dx_o, n_o, dyo_o, nr_o, ur_o, act_o, sact_o, dl_o,
    x_a, dy_a, n_a, u_a, ids, wg, wu, wd, sg, su, sd, nr, ur, act, sact, dl,
    part, recv, o_all, dn_all, yb, dgb, pjb, tgt_v, g_v, df_v, dnr_v,
    xl, wl, sl, ids_s, ids_r, xs, xr, zs, zr, es, er, ys, yr, dgs, dgr, pjs, pjr, outs,
):
    z = lax.axis_index("etp")
    e = lax.axis_index("ep")
    e_y, e_c, e_d = e ^ 2, e ^ 1, e ^ 3
    peers = (e_y, e_c, e_d)
    is_end = (z == 0) | (z == 3)
    is_mid = (z == 1) | (z == 2)
    hs = z // 3

    def rows(j):
        return pl.ds(pl.multiple_of(j * TL, TL), TL)

    mine = rows(e)
    lx = pltpu.make_async_copy(x_h, x_a.at[mine], xl.at[0])
    ldy = pltpu.make_async_copy(dy_h, dy_a.at[mine], xl.at[1])
    lx.start()
    ldy.start()
    shared_loads = [pltpu.make_async_copy(a, b, sl.at[k]) for k, (a, b) in enumerate(((sg_h, sg), (su_h, su), (sd_h, sd)))]
    for c in shared_loads:
        c.start()

    def wload(k, i):
        src, dst = ((wg_h, wg), (wu_h, wu), (wd_h, wd))[k]
        return pltpu.make_async_copy(src.at[i], dst.at[i], wl.at[k, i])

    ids[e] = jnp.zeros((8, TL), F32)
    ids[e, 0:1, :] = prim_v[...].astype(F32)
    ids[e, 1:2, :] = alt_v[...].astype(F32)

    barrier = pltpu.get_barrier_semaphore()
    for q in peers:
        pl.semaphore_signal(barrier, inc=1, device_id={"ep": q}, device_id_type=MESH)
    for k in range(1, 4):
        pl.semaphore_signal(barrier, inc=1, device_id={"etp": lax.rem(z + k, 4)}, device_id_type=MESH)
    pl.semaphore_wait(barrier, 6)

    def rcopy(src, dst, s, r, dev):
        return pltpu.make_async_remote_copy(src_ref=src, dst_ref=dst, send_sem=s, recv_sem=r, device_id=dev, device_id_type=MESH)

    ids_c = [rcopy(ids.at[e], ids.at[e], ids_s.at[k], ids_r.at[k], {"ep": peers[k]}) for k in range(3)]
    for c in ids_c:
        c.start()
    lx.wait()
    x_c, relays = [], []
    for k, buf in enumerate((x_a, dy_a)):
        if k == 1:
            ldy.wait()
        pair = [
            rcopy(buf.at[mine], buf.at[mine], xs.at[k, 0], xr.at[k, 0], {"ep": e_y}),
            rcopy(buf.at[mine], buf.at[mine], xs.at[k, 1], xr.at[k, 1], {"ep": e_c}),
        ]
        for c in pair:
            c.start()
        x_c.append(pair)
        relays.append(rcopy(buf.at[rows(e_y)], buf.at[rows(e_y)], xs.at[k, 2], xr.at[k, 2], {"ep": e_c}))

    def load_body(i, _):
        for k in range(3):
            wload(k, i).start()
        return 0

    lax.fori_loop(0, EL, load_body, 0)

    def line_copy(d, m):
        return rcopy(part.at[d, m], recv.at[d, m], zs.at[d, m], zr.at[d, m], {"etp": jnp.clip(z - 1 + 2 * d, 0, 3)})

    def source_send(m):
        @pl.when(z == 3)
        def _():
            line_copy(0, m).start()

        @pl.when(z == 0)
        def _():
            line_copy(1, m).start()

    def take(d, m):
        line_copy(d, m).wait_recv()
        part[d, m] = part[d, m] + recv[d, m]

    def forward(hop, m):
        @pl.when(is_mid)
        def _():
            d = (2 - z) if hop == 1 else (z - 1)
            take(d, m)
            line_copy(d, m).start()

    def norm(xw):
        inv = lax.rsqrt(jnp.mean(xw * xw, axis=1, keepdims=True) + EPS)
        return inv, (xw * inv).astype(BF16)

    for c in shared_loads:
        c.wait()

    def shared_acts(n, dy):
        a = dot(n, sg[...])
        b = dot(n, su[...])
        h = glu(a, b)
        dg_, du_ = glu_grads(dot_t(dy, sd[...]), a, b)
        return h, dg_, du_

    _, n_own = norm(x_a[mine, :].astype(F32))
    h_s, da_s, db_s = shared_acts(n_own, dy_a[mine, :])
    s_part = dot(h_s, sd[...])
    for k in range(4):
        part[0, k] = s_part[k * MR : (k + 1) * MR, :HD]
        part[1, k] = s_part[k * MR : (k + 1) * MR, HD:]
    dns_part = dot_t(da_s, sg[...]) + dot_t(db_s, su[...])
    for k in range(4):
        part[0, 4 + k] = dns_part[k * MR : (k + 1) * MR, :HD]
        part[1, 4 + k] = dns_part[k * MR : (k + 1) * MR, HD:]
    for m in range(8):
        source_send(m)

    forward(1, 0)

    for c in ids_c:
        c.wait_recv()
    x_c[0][0].wait_recv()
    relays[0].start()
    x_c[0][1].wait_recv()
    relays[0].wait_recv()

    def norm_body(j, _):
        _, n = norm(x_a[rows(j), :].astype(F32))
        n_a[rows(j), :] = n
        return 0

    lax.fori_loop(0, NEP, norm_body, 0)
    forward(1, 1)

    logits = dot(n_a[...], wr_v[...])
    ex = jnp.exp(logits - jnp.max(logits, axis=1, keepdims=True))
    probs = ex / jnp.sum(ex, axis=1, keepdims=True)
    cols = []
    for j in range(NEP):
        block = jnp.concatenate([ids[j], jnp.zeros((TL - 8, TL), F32)], axis=0)
        cols.append(jnp.transpose(block)[:, 0:2])
    idc = jnp.concatenate(cols, axis=0)
    prim, alt = idc[:, 0:1], idc[:, 1:2]
    iota_e = lax.broadcasted_iota(jnp.int32, (T, E), 1).astype(F32)
    one_p = jnp.where(prim == iota_e, 1.0, 0.0)
    earlier = jnp.where(
        lax.broadcasted_iota(jnp.int32, (T, T), 0) > lax.broadcasted_iota(jnp.int32, (T, T), 1), 1.0, 0.0
    ).astype(BF16)
    rank = jnp.sum(dot(earlier, one_p.astype(BF16)) * one_p, axis=1, keepdims=True)
    over = jnp.where(rank < CAP, 0.0, 1.0)
    kept = jnp.minimum(jnp.sum(one_p, axis=0, keepdims=True), float(CAP))
    one_a = jnp.where(alt == iota_e, 1.0, 0.0) * over
    slot_a = jnp.sum((dot(earlier, one_a.astype(BF16)) + kept) * one_a, axis=1, keepdims=True)
    keep_a = over * jnp.where(slot_a < CAP, 1.0, 0.0)
    one_s = one_p * (1.0 - over) + one_a * keep_a
    slot = (1.0 - over) * rank + keep_a * slot_a
    eid = jnp.sum(one_s * iota_e, axis=1, keepdims=True)
    has = (1.0 - over) + keep_a
    tgt_v[...] = jnp.where(has > 0.5, eid * CAP + slot, -1.0)
    g_v[...] = jnp.sum(probs * one_s, axis=1, keepdims=True)
    df_v[...] = one_s - probs

    base = (e * (EL * CAP)).astype(F32)
    pick = jnp.where(
        tgt_v[...] - base == lax.broadcasted_iota(jnp.int32, (T, EL * CAP), 1).astype(F32), 1.0, 0.0
    ).astype(BF16)
    nr[...] = tdot(pick, n_a[...]).astype(BF16)
    forward(1, 2)
    forward(2, 0)
    forward(1, 3)
    forward(2, 1)

    x_c[1][0].wait_recv()
    relays[1].start()
    x_c[1][1].wait_recv()
    relays[1].wait_recv()

    def u_body(j, _):
        u_a[rows(j), :] = (g_v[rows(j), :] * dy_a[rows(j), :].astype(F32)).astype(BF16)
        return 0

    lax.fori_loop(0, NEP, u_body, 0)
    forward(1, 4)
    forward(2, 2)
    ur[...] = tdot(pick, u_a[...]).astype(BF16)

    def pair_body(k, _):
        for half in range(2):
            i = 2 * k + half
            for w in range(3):
                wload(w, i).wait()
            sl16 = pl.ds(pl.multiple_of(i * CAP, CAP), CAP)
            n_i, u_i = nr[sl16, :], ur[sl16, :]
            a = dot(n_i, wg[i])
            b = dot(n_i, wu[i])
            h = glu(a, b)
            da, db = glu_grads(dot_t(u_i, wd[i]), a, b)
            act[0, sl16, :] = h
            act[1, sl16, :] = da
            act[2, sl16, :] = db
            o = dot(h, wd[i])
            r16 = slice(half * CAP, (half + 1) * CAP)
            part[0, 8 + k, r16, :] = o[:, :HD]
            part[1, 8 + k, r16, :] = o[:, HD:]
            dn = dot_t(da, wg[i]) + dot_t(db, wu[i])
            part[0, 13 + k, r16, :] = dn[:, :HD]
            part[1, 13 + k, r16, :] = dn[:, HD:]
        source_send(8 + k)

        @pl.when(k < 3)
        def _():
            forward(1, 5 + k)

        forward(2, 3 + k)
        return 0

    lax.fori_loop(0, EL // 2, pair_body, 0)
    for m in range(13, 18):
        source_send(m)

    stores = [
        pltpu.make_async_copy(n_a, n_o, outs.at[0]),
        pltpu.make_async_copy(dy_a, dyo_o, outs.at[1]),
        pltpu.make_async_copy(nr, nr_o, outs.at[2]),
        pltpu.make_async_copy(ur, ur_o, outs.at[3]),
        pltpu.make_async_copy(act, act_o, outs.at[4]),
    ]
    for c in stores:
        c.start()

    def fwd_body(m, _):
        forward(1, m)
        forward(2, m)
        return 0

    lax.fori_loop(8, NM, fwd_body, 0)

    def sact_body(j, _):
        h, da, db = shared_acts(n_a[rows(j), :], dy_a[rows(j), :])
        sact[0, rows(j), :] = h
        sact[1, rows(j), :] = da
        sact[2, rows(j), :] = db
        return 0

    lax.fori_loop(0, NEP, sact_body, 0)
    st = pltpu.make_async_copy(sact, sact_o, outs.at[5])
    st.start()
    stores.append(st)

    def exchange(t, k, p):
        buf = (o_all, dn_all)[t]
        return rcopy(buf.at[e, k], buf.at[e, k], es.at[t, k, p], er.at[t, k, p], {"ep": peers[p]})

    lanes = pl.ds(pl.multiple_of(hs * HD, 128), HD)

    def place(n_rows, start):
        t_col = tgt_v[pl.ds(start, n_rows), :]
        return jnp.where(
            t_col == lax.broadcasted_iota(jnp.int32, (n_rows, E * CAP), 1).astype(F32), 1.0, 0.0
        ).astype(BF16)

    def col_to_row(col):
        return jnp.transpose(jnp.broadcast_to(col, (TL, TL)))[0:1, :]

    def dg_copy(h, k):
        return rcopy(dgb.at[h], dgb.at[h], dgs.at[k], dgr.at[h], {"etp": lax.rem(z + k + 1, 4)})

    def pj_copy():
        return rcopy(pjb.at[hs], pjb.at[hs], pjs.at[0], pjr.at[0], {"etp": 3 - z})

    def end_take(m, _):
        take(hs, m)
        return 0

    def end_take_o(k, _):
        take(hs, 8 + k)
        o_all[e, k] = part[hs, 8 + k].astype(BF16)
        for p in range(3):
            exchange(0, k, p).start()
        return 0

    def end_take_dn(k, _):
        take(hs, 13 + k)
        dn_all[e, k] = part[hs, 13 + k].astype(BF16)
        for p in range(3):
            exchange(1, k, p).start()
        return 0

    def wait_exchange(t):
        def body(k, _):
            for p in range(3):
                exchange(t, k, p).wait_recv()
            return 0

        lax.fori_loop(0, EL // 2, body, 0)

    def relay_copy(t, h, c):
        return rcopy(yb.at[t, h, c], yb.at[t, h, c], ys.at[t, h, c], yr.at[t, h, c], {"etp": jnp.clip(z + 1 - 2 * h, 0, 3)})

    def relay_start(t):
        for c in range(NC):
            relay_copy(t, hs, c).start()

    @pl.when(is_end)
    def _():
        lax.fori_loop(0, 8, end_take, 0)
        lax.fori_loop(0, EL // 2, end_take_o, 0)
        wait_exchange(0)
        o_flat = o_all[...].reshape(E * CAP, HD)
        for j in range(NEP):
            tok = dot(place(TL, j * TL), o_flat)
            prod = dy_a[j * TL : (j + 1) * TL, lanes].astype(F32) * tok
            dgb[hs, 0:1, j * TL : (j + 1) * TL] = col_to_row(jnp.sum(prod, axis=1, keepdims=True))
        for k in range(3):
            dg_copy(hs, k).start()
        tok = dot(place(TL, pl.multiple_of(e * TL, TL)), o_flat)
        s_own = part[hs, 0:4].reshape(TL, HD)
        y = (x_a[mine, lanes].astype(F32) + s_own + g_v[mine, :] * tok).astype(BF16)
        for c in range(NC):
            yb[0, hs, c] = y[c * CR : (c + 1) * CR, :]
        relay_start(0)

    @pl.when(z != 0)
    def _():
        dg_copy(0, 0).wait_recv()

    @pl.when(z != 3)
    def _():
        dg_copy(1, 0).wait_recv()

    for j in range(NEP):
        row = dgb[0, 0:1, j * TL : (j + 1) * TL] + dgb[1, 0:1, j * TL : (j + 1) * TL]
        dg_col = jnp.transpose(jnp.broadcast_to(row, (TL, TL)))[:, 0:1]
        sl_j = slice(j * TL, (j + 1) * TL)
        dl[sl_j, :] = (dg_col * g_v[sl_j, :] * df_v[sl_j, :]).astype(BF16)
    st = pltpu.make_async_copy(dl, dl_o, outs.at[6])
    st.start()
    stores.append(st)

    def relay_through(t):
        for c in range(NC):
            for h in range(2):
                @pl.when(z != 3 * h)
                def _(h=h, c=c):
                    relay_copy(t, h, c).wait_recv()

                @pl.when(is_mid)
                def _(h=h, c=c):
                    relay_copy(t, h, c).start()

    @pl.when(is_mid)
    def _():
        relay_through(0)

    @pl.when(is_end)
    def _():
        dn_r = dot_t(dl[mine, :], wr_v[...])
        dnr_v[0] = dn_r[:, :HD]
        dnr_v[1] = dn_r[:, HD:]
        lax.fori_loop(0, EL // 2, end_take_dn, 0)
        wait_exchange(1)
        tok = dot(place(TL, pl.multiple_of(e * TL, TL)), dn_all[...].reshape(E * CAP, HD))
        dn = part[hs, 4:8].reshape(TL, HD) + dnr_v[hs] + tok
        dnr_v[hs] = dn
        xh = x_a[mine, lanes].astype(F32)
        pjb[hs, 0:1, :] = col_to_row(jnp.sum(dn * xh, axis=1, keepdims=True))
        pj_copy().start()
        inv, _ = norm(x_a[mine, :].astype(F32))
        pj_copy().wait_recv()
        row = pjb[0, 0:1, :] + pjb[1, 0:1, :]
        proj = jnp.transpose(jnp.broadcast_to(row, (TL, TL)))[:, 0:1] * (1.0 / D)
        dx = (dy_a[mine, lanes].astype(F32) + inv * dnr_v[hs] - x_a[mine, lanes].astype(F32) * (inv * inv * inv) * proj).astype(BF16)
        for c in range(NC):
            yb[1, hs, c] = dx[c * CR : (c + 1) * CR, :]
        relay_start(1)

    @pl.when(is_end)
    def _():
        relay_through(0)

    def out_copies(t, out):
        cs = []
        for h in range(2):
            for c in range(NC):
                cs.append(pltpu.make_async_copy(yb.at[t, h, c], out.at[pl.ds(c * CR, CR), pl.ds(h * HD, HD)], outs.at[7 + t * 2 * NC + h * NC + c]))
        return cs

    oc = out_copies(0, y_o)
    for c in oc:
        c.start()
    stores += oc
    relay_through(1)
    oc = out_copies(1, dx_o)
    for c in oc:
        c.start()
    stores += oc

    for c in ids_c:
        c.wait_send()
    for k in range(2):
        for c in x_c[k]:
            c.wait_send()
        relays[k].wait_send()

    def line_drain(m, _):
        @pl.when(z != 0)
        def _():
            line_copy(0, m).wait_send()

        @pl.when(z != 3)
        def _():
            line_copy(1, m).wait_send()

        return 0

    lax.fori_loop(0, NM, line_drain, 0)

    @pl.when(is_end)
    def _():
        def drain(k, _):
            for t in range(2):
                for p in range(3):
                    exchange(t, k, p).wait_send()
            return 0

        lax.fori_loop(0, EL // 2, drain, 0)
        for k in range(3):
            dg_copy(hs, k).wait_send()
        pj_copy().wait_send()

    for t in range(2):
        for c in range(NC):
            @pl.when(z != 3)
            def _(t=t, c=c):
                relay_copy(t, 0, c).wait_send()

            @pl.when(z != 0)
            def _(t=t, c=c):
                relay_copy(t, 1, c).wait_send()

    for c in stores:
        c.wait()


def grads_kernel(nr, ur, act, gg, gu, gd):
    n, u = nr[...], ur[...]
    gg[0] = tdot(n, act[1])
    gu[0] = tdot(n, act[2])
    gd[0] = tdot(act[0], u)


def solution(mesh):
    tok = P(("dp", "ep"), None)
    ids = P(("dp", "ep"))
    in_specs = (tok, tok, ids, ids, P(None, None), P("ep", None, "etp"), P("ep", None, "etp"), P("ep", "etp", None), P(None, "etp"), P(None, "etp"), P("etp", None))
    out_specs = (tok, tok, P(("dp", "ep"), None, "etp"), P(("dp", "ep"), None, "etp"), P(("dp", "ep"), "etp", None), P("dp", "etp"), P("dp", "etp"), P(("dp", "etp"), None), P("dp", None))
    any_ = pl.BlockSpec(memory_space=pl.ANY)
    vmem = pl.BlockSpec(memory_space=pltpu.VMEM)
    dma = pltpu.SemaphoreType.DMA

    def sds(shape, dtype):
        return jax.ShapeDtypeStruct(shape, dtype)

    def step(x, dy, prim, alt, wr, eg, eu, ed, sg, su, sd):
        outs = [
            sds((TL, D), BF16), sds((TL, D), BF16), sds((T, D), BF16), sds((T, D), BF16),
            sds((EL * CAP, D), BF16), sds((EL * CAP, D), BF16), sds((3, EL * CAP, W), BF16), sds((3, T, W), BF16), sds((T, E), BF16),
        ]
        V = pltpu.VMEM
        scratch = [
            V((T, D), BF16), V((T, D), BF16), V((T, D), BF16), V((T, D), BF16), V((NEP, 8, TL), F32),
            V((EL, D, W), BF16), V((EL, D, W), BF16), V((EL, W, D), BF16), V((D, W), BF16), V((D, W), BF16), V((W, D), BF16),
            V((EL * CAP, D), BF16), V((EL * CAP, D), BF16), V((3, EL * CAP, W), BF16), V((3, T, W), BF16), V((T, E), BF16),
            V((2, NM, MR, HD), F32), V((2, NM, MR, HD), F32), V((NEP, EL // 2, MR, HD), BF16), V((NEP, EL // 2, MR, HD), BF16),
            V((2, 2, NC, CR, HD), BF16), V((2, 8, T), F32), V((2, 8, TL), F32), V((T, 1), F32), V((T, 1), F32), V((T, E), F32), V((2, TL, HD), F32),
            dma((2,)), dma((3, EL)), dma((3,)), dma((3,)), dma((3,)), dma((2, 3)), dma((2, 3)), dma((2, NM)), dma((2, NM)),
            dma((2, EL // 2, 3)), dma((2, EL // 2, 3)), dma((2, 2, NC)), dma((2, 2, NC)), dma((3,)), dma((2,)), dma((1,)), dma((1,)), dma((7 + 4 * NC,)),
        ]
        y, dx, n_a, dy_a, nr, ur, act, sact, dl = pl.pallas_call(
            line_kernel,
            name="line",
            out_shape=outs,
            in_specs=[any_, any_, vmem, vmem, vmem] + [any_] * 6,
            out_specs=[any_] * 9,
            scratch_shapes=scratch,
            compiler_params=pltpu.CompilerParams(collective_id=0, has_side_effects=True, vmem_limit_bytes=60 * 1024 * 1024),
        )(x, dy, prim.reshape(1, TL), alt.reshape(1, TL), wr, eg, eu, ed, sg, su, sd)

        gg, gu, gd = pl.pallas_call(
            grads_kernel,
            name="grads",
            grid=(EL,),
            out_shape=[sds((EL, D, W), F32), sds((EL, D, W), F32), sds((EL, W, D), F32)],
            in_specs=[pl.BlockSpec((CAP, D), lambda i: (i, 0)), pl.BlockSpec((CAP, D), lambda i: (i, 0)), pl.BlockSpec((3, CAP, W), lambda i: (0, i, 0))],
            out_specs=[pl.BlockSpec((1, D, W), lambda i: (i, 0, 0)), pl.BlockSpec((1, D, W), lambda i: (i, 0, 0)), pl.BlockSpec((1, W, D), lambda i: (i, 0, 0))],
            compiler_params=pltpu.CompilerParams(vmem_limit_bytes=40 * 1024 * 1024),
        )(nr, ur, act)
        g_sg = jnp.einsum("td,tf->df", n_a, sact[1], preferred_element_type=F32)
        g_su = jnp.einsum("td,tf->df", n_a, sact[2], preferred_element_type=F32)
        g_sd = jnp.einsum("tf,td->fd", sact[0], dy_a, preferred_element_type=F32)
        g_r = jnp.einsum("td,te->de", n_a, dl, preferred_element_type=F32)
        return y, dx, gg, gu, gd, g_sg, g_su, g_sd, g_r

    return jax.shard_map(step, mesh=mesh, in_specs=in_specs, out_specs=out_specs, check_vma=False)
```

time: 297 us -> 154 us (0.52)
  Pallas kernels: 0 us -> 143 us
  blocking collectives: 107 us -> 0 us
  waiting for transfers between devices: 85.1 us -> 0 us
  matrix products: 33.7 us -> 6.92 us
  local copies, waits for them, and re-layouts: 23.1 us -> 3.59 us
  other arithmetic: 17.2 us -> 0 us
  starting transfers between devices: 15.2 us -> 0 us
  between operations: 15.1 us -> 0.69 us
    pallas_call x0 -> x2, Pallas kernels: none -> 143 us  [the longest x1 133 us: step(): pl.pallas_call(line_kernel, name='line', out_shape=outs, in_specs=[any_,...]
    psum x1 -> x0, blocking collectives: 74.7 us -> none  [local_step(): lax.psum(jnp.einsum('ecf,efd->ecd', hidden, exp_down, preferred_element_t...]
    psum x2 -> x0, waiting for transfers between devices: 45.4 us -> none  [the longest x1 45.4 us: local_step(): lax.psum(jnp.einsum('td,tf->df', normed, sh_d_gate, preferred_element_typ...]
    all_to_all x4 -> x0, waiting for transfers between devices: 39.7 us -> none  [the longest x2 23.5 us: send_back(): lax.all_to_all(flat_rows.reshape(ep_size, tok_local, model_dim), 'ep', 0,...]
    dot_general x21 -> x4, matrix products: 33.7 us -> 6.92 us  [the longest x1 2.65 us: step(): g_r = jnp.einsum('td,te->de', n_a, dl, preferred_element_type=F32)]
    all_gather x2 -> x0, blocking collectives: 21.3 us -> none  [the longest x1 16.2 us: local_step(): all_assign = lax.all_gather(assign, 'ep', tiled=True)]
    all_to_all x4 -> x0, starting transfers between devices: 15.2 us -> none  [the longest x2 8.04 us: send_out(): lax.all_to_all(sent_rows, 'ep', 0, 0, tiled=True)]
    unnamed x2 -> x0, blocking collectives: 10.7 us -> none
  transfers between devices with their start and end apart: 6 -> 0, of which waited for: 4 -> 0; matrix products, arithmetic and copies ran while one was open for 18% -> 0% of each run, Pallas kernels for 0% -> 0%
where the time goes in v1:
time: 154 us
  Pallas kernels  143 us (93%)
  matrix products  6.92 us (4%)
  local copies, waits for them, and re-layouts  3.59 us (2%)
    pallas_call x1, Pallas kernels, step(): pl.pallas_call(line_kernel, name='line', out_shape=outs, in_specs=[any_,...  133 us
    pallas_call x1, Pallas kernels, step(): pl.pallas_call(grads_kernel, name='grads', grid=(EL,), out_shape=[sds((EL...  9.67 us
    unnamed x19, local copies, waits for them, and re-layouts  3.59 us

profile of v1, /device:TPU:0, one launch (start us, length us, event | category | flops | bytes accessed | tf_op | source)
XLA Modules:
  0.0 153.7 jit_solution(5228307088388232343)
XLA Ops:
  0.6 1.8 %copy.20.wr_v = bf16[1536,40]{1,0:T(8,128)(2,1)} copy(bf16[1536,40]{0,1:T(8,128)(2,1)} %param.15) | data formatting | bytes 245760 | tf_op args[4]
  2.5 132.9 %line.1 = (bf16[128,1536]{1,0:T(8,128)(2,1)}, bf16[128,1536]{1,0:T(8,128)(2,1)}, bf16[512,1536]{1,0:T(8,128)(2,1)}, bf16[512,1536]{1,0:T(8,128)(2,1)}, bf16[160,...) custom-call(bf16[128,1536]{1,0:T(8,128)(2,1)} %x_h.1, ...), custom_call_target="tpu_custom_call" | custom-call | tf_op jit(solution)/shard_map/line/pallas_call | solution.py:532
  135.3 0.0 copy-start.4
  135.3 0.0 copy-start.5
  135.3 2.7 %fusion.9 = f32[1536,40]{0,1:T(8,128)} fusion(bf16[512,1536]{1,0:T(8,128)(2,1)} %get-tuple-element.29, bf16[512,40]{1,0:T(8,128)(2,1)} %get-tuple-element.32), kind=kOutput, calls=%fused_computation.9 | convolution fusion | flops 62914560 | bytes 1859584 | tf_op jit(solution)/shard_map/td,te->de/dot_general | solution.py:554
  138.0 0.0 copy-done.4
  138.0 0.0 copy-done.5
  138.0 0.0 copy-start.3
  138.0 1.3 fusion
  139.3 0.2 copy-done.3
  139.5 1.5 fusion.2
  141.0 0.0 copy-start
  141.0 0.0 copy-start.1
  141.0 0.0 copy-start.2
  141.0 0.0 copy-start.7
  141.0 0.0 copy-start.6
  141.0 1.5 fusion.4
  142.5 0.0 copy-done
  142.5 0.0 copy-done.1
  142.5 0.0 copy-done.2
  142.5 9.7 %grads.1 = (f32[10,1536,128]{2,1,0:T(8,128)}, f32[10,1536,128]{2,1,0:T(8,128)}, f32[10,128,1536]{2,1,0:T(8,128)}) custom-call(bf16[160,1536]{1,0:T(8,128)(2,1)S(1)} %copy-done, bf16[160,1536]{1,0:T(8,128)(2,1)S(1)} %copy-done.1, bf16[3,160,128]{2,1,0:T(8,128)(2,1)S(1)} %copy-done.2), custom_call_target="tpu_custom_call" | custom-call | tf_op jit(solution)/shard_map/grads/pallas_call | solution.py:542
  152.2 0.0 copy-done.7
  152.2 0.7 copy.23
  153.0 0.0 copy-done.6
  153.0 0.7 copy.24
Async XLA Ops:
  135.3 2.7 %copy-start.4 = (bf16[512,1536]{1,0:T(8,128)(2,1)S(1)}, bf16[512,1536]{1,0:T(8,128)(2,1)}, u32[]{:S(2)}) copy-start(bf16[512,1536]{1,0:T(8,128)(2,1)} %get-tuple-element.31) | copy-start | bytes 4718596
  135.3 2.7 %copy-start.5 = (bf16[3,512,128]{2,1,0:T(8,128)(2,1)S(1)}, bf16[3,512,128]{2,1,0:T(8,128)(2,1)}, u32[]{:S(2)}) copy-start(bf16[3,512,128]{2,1,0:T(8,128)(2,1)} %get-tuple-element.30) | copy-start | bytes 1179652
  138.0 1.5 copy-start.3
  141.0 1.5 copy-start
  141.0 1.5 copy-start.1
  141.0 1.5 copy-start.2
  141.0 11.2 %copy-start.7 = (bf16[128,1536]{1,0:T(8,128)(2,1)S(1)}, bf16[128,1536]{1,0:T(8,128)(2,1)}, u32[]{:S(2)}) copy-start(bf16[128,1536]{1,0:T(8,128)(2,1)} %get-tuple-element.42) | copy-start | bytes 1179652
  141.0 11.9 %copy-start.6 = (bf16[128,1536]{1,0:T(8,128)(2,1)S(1)}, bf16[128,1536]{1,0:T(8,128)(2,1)}, u32[]{:S(2)}) copy-start(bf16[128,1536]{1,0:T(8,128)(2,1)} %get-tuple-element.43) | copy-start | bytes 1179652

commit v2 on v1

--- a/solution.py
+++ b/solution.py
@@ -53,7 +53,7 @@
     x_h, dy_h, prim_v, alt_v, wr_v, wg_h, wu_h, wd_h, sg_h, su_h, sd_h,
     y_o, dx_o, n_o, dyo_o, nr_o, ur_o, act_o, sact_o, dl_o,
     x_a, dy_a, n_a, u_a, ids, wg, wu, wd, sg, su, sd, nr, ur, act, sact, dl,
-    part, recv, o_all, dn_all, yb, dgb, pjb, tgt_v, g_v, df_v, dnr_v,
+    part, recv, o_all, dn_all, yb, dgb, pjb, tgt_v, g_v, df_v, dnr_v, ab,
     xl, wl, sl, ids_s, ids_r, xs, xr, zs, zr, es, er, ys, yr, dgs, dgr, pjs, pjr, outs,
 ):
     z = lax.axis_index("etp")
@@ -169,6 +169,9 @@
         source_send(m)
 
     forward(1, 0)
+    forward(1, 1)
+    forward(1, 2)
+    forward(2, 0)
 
     for c in ids_c:
         c.wait_recv()
@@ -183,9 +186,10 @@
         return 0
 
     lax.fori_loop(0, NEP, norm_body, 0)
-    forward(1, 1)
-
-    logits = dot(n_a[...], wr_v[...])
+    forward(1, 3)
+    forward(2, 1)
+
+    logits = dot_t(n_a[...], wr_v[...])
     ex = jnp.exp(logits - jnp.max(logits, axis=1, keepdims=True))
     probs = ex / jnp.sum(ex, axis=1, keepdims=True)
     cols = []
@@ -218,59 +222,64 @@
         tgt_v[...] - base == lax.broadcasted_iota(jnp.int32, (T, EL * CAP), 1).astype(F32), 1.0, 0.0
     ).astype(BF16)
     nr[...] = tdot(pick, n_a[...]).astype(BF16)
-    forward(1, 2)
-    forward(2, 0)
-    forward(1, 3)
-    forward(2, 1)
-
-    x_c[1][0].wait_recv()
-    relays[1].start()
-    x_c[1][1].wait_recv()
-    relays[1].wait_recv()
-
-    def u_body(j, _):
-        u_a[rows(j), :] = (g_v[rows(j), :] * dy_a[rows(j), :].astype(F32)).astype(BF16)
-        return 0
-
-    lax.fori_loop(0, NEP, u_body, 0)
     forward(1, 4)
     forward(2, 2)
-    ur[...] = tdot(pick, u_a[...]).astype(BF16)
-
-    def pair_body(k, _):
+    forward(1, 5)
+    forward(2, 3)
+
+    def fwd_pair(k, _):
         for half in range(2):
             i = 2 * k + half
             for w in range(3):
                 wload(w, i).wait()
             sl16 = pl.ds(pl.multiple_of(i * CAP, CAP), CAP)
-            n_i, u_i = nr[sl16, :], ur[sl16, :]
+            n_i = nr[sl16, :]
             a = dot(n_i, wg[i])
             b = dot(n_i, wu[i])
             h = glu(a, b)
-            da, db = glu_grads(dot_t(u_i, wd[i]), a, b)
+            ab[0, sl16, :] = a
+            ab[1, sl16, :] = b
             act[0, sl16, :] = h
-            act[1, sl16, :] = da
-            act[2, sl16, :] = db
             o = dot(h, wd[i])
             r16 = slice(half * CAP, (half + 1) * CAP)
             part[0, 8 + k, r16, :] = o[:, :HD]
             part[1, 8 + k, r16, :] = o[:, HD:]
+        source_send(8 + k)
+        return 0
+
+    lax.fori_loop(0, EL // 2, fwd_pair, 0)
+    forward(1, 6)
+    forward(2, 4)
+    forward(1, 7)
+    forward(2, 5)
+
+    x_c[1][0].wait_recv()
+    relays[1].start()
+    x_c[1][1].wait_recv()
+    relays[1].wait_recv()
+
+    def u_body(j, _):
+        u_a[rows(j), :] = (g_v[rows(j), :] * dy_a[rows(j), :].astype(F32)).astype(BF16)
+        return 0
+
+    lax.fori_loop(0, NEP, u_body, 0)
+    ur[...] = tdot(pick, u_a[...]).astype(BF16)
+
+    def pair_body(k, _):
+        for half in range(2):
+            i = 2 * k + half
+            sl16 = pl.ds(pl.multiple_of(i * CAP, CAP), CAP)
+            da, db = glu_grads(dot_t(ur[sl16, :], wd[i]), ab[0, sl16, :], ab[1, sl16, :])
+            act[1, sl16, :] = da
+            act[2, sl16, :] = db
+            r16 = slice(half * CAP, (half + 1) * CAP)
             dn = dot_t(da, wg[i]) + dot_t(db, wu[i])
             part[0, 13 + k, r16, :] = dn[:, :HD]
             part[1, 13 + k, r16, :] = dn[:, HD:]
-        source_send(8 + k)
-
-        @pl.when(k < 3)
-        def _():
-            forward(1, 5 + k)
-
-        forward(2, 3 + k)
+        source_send(13 + k)
         return 0
 
     lax.fori_loop(0, EL // 2, pair_body, 0)
-    for m in range(13, 18):
-        source_send(m)
-
     stores = [
         pltpu.make_async_copy(n_a, n_o, outs.at[0]),
         pltpu.make_async_copy(dy_a, dyo_o, outs.at[1]),
@@ -283,10 +292,12 @@
 
     def fwd_body(m, _):
         forward(1, m)
-        forward(2, m)
+        forward(2, m - 2)
         return 0
 
     lax.fori_loop(8, NM, fwd_body, 0)
+    forward(2, NM - 2)
+    forward(2, NM - 1)
 
     def sact_body(j, _):
         h, da, db = shared_acts(n_a[rows(j), :], dy_a[rows(j), :])
@@ -390,16 +401,27 @@
     st.start()
     stores.append(st)
 
+    def relay_wait(t, h, c):
+        relay_copy(t, h, c).wait_recv()
+
     def relay_through(t):
-        for c in range(NC):
-            for h in range(2):
-                @pl.when(z != 3 * h)
-                def _(h=h, c=c):
-                    relay_copy(t, h, c).wait_recv()
-
-                @pl.when(is_mid)
-                def _(h=h, c=c):
-                    relay_copy(t, h, c).start()
+        def hop(n, c):
+            h = (z - 1) if n == 1 else (2 - z)
+            relay_wait(t, h, c)
+            relay_copy(t, h, c).start()
+
+        @pl.when(is_mid)
+        def _():
+            for c in range(NC + 2):
+                if c < NC:
+                    hop(1, c)
+                if c >= 2:
+                    hop(2, c - 2)
+
+        @pl.when(is_end)
+        def _():
+            for c in range(NC):
+                relay_wait(t, 1 - hs, c)
 
     @pl.when(is_mid)
     def _():
@@ -407,7 +429,7 @@
 
     @pl.when(is_end)
     def _():
-        dn_r = dot_t(dl[mine, :], wr_v[...])
+        dn_r = dot(dl[mine, :], wr_v[...])
         dnr_v[0] = dn_r[:, :HD]
         dnr_v[1] = dn_r[:, HD:]
         lax.fori_loop(0, EL // 2, end_take_dn, 0)
@@ -495,11 +517,49 @@
         c.wait()
 
 
-def grads_kernel(nr, ur, act, gg, gu, gd):
-    n, u = nr[...], ur[...]
-    gg[0] = tdot(n, act[1])
-    gu[0] = tdot(n, act[2])
-    gd[0] = tdot(act[0], u)
+def grads_kernel(nr, ur, act, n_h, dy_h, sact, dl, y_h, dx_h, gg, gu, gd, gsg_h, gsu_h, gsd_h, gr_h, yo_h, dxo_h, n, dy, yx, gs, gsd, gr, li, so):
+    i = pl.program_id(0)
+    loads = [pltpu.make_async_copy(a, b, li.at[k]) for k, (a, b) in enumerate(((n_h, n), (dy_h, dy), (y_h, yx.at[0]), (dx_h, yx.at[1])))]
+    pairs = ((gs.at[0], gsg_h), (gs.at[1], gsu_h), (gsd, gsd_h), (gr, gr_h), (yx.at[0], yo_h), (yx.at[1], dxo_h))
+    stores = [pltpu.make_async_copy(a, b, so.at[k]) for k, (a, b) in enumerate(pairs)]
+
+    @pl.when(i == 0)
+    def _():
+        for c in loads:
+            c.start()
+
+    @pl.when(i == 2)
+    def _():
+        for c in loads:
+            c.wait()
+        for c in stores[4:]:
+            c.start()
+        gs[0] = tdot(n[...], sact[1])
+        stores[0].start()
+
+    @pl.when(i == 3)
+    def _():
+        gs[1] = tdot(n[...], sact[2])
+        stores[1].start()
+
+    @pl.when(i == 4)
+    def _():
+        gsd[...] = tdot(sact[0], dy[...])
+        stores[2].start()
+
+    @pl.when(i == 5)
+    def _():
+        gr[...] = tdot(dl[...], n[...])
+        stores[3].start()
+
+    @pl.when(i == EL - 1)
+    def _():
+        for c in stores:
+            c.wait()
+
+    gg[0] = tdot(nr[...], act[1])
+    gu[0] = tdot(nr[...], act[2])
+    gd[0] = tdot(act[0], ur[...])
 
 
 def solution(mesh):
@@ -525,7 +585,7 @@
             V((EL, D, W), BF16), V((EL, D, W), BF16), V((EL, W, D), BF16), V((D, W), BF16), V((D, W), BF16), V((W, D), BF16),
             V((EL * CAP, D), BF16), V((EL * CAP, D), BF16), V((3, EL * CAP, W), BF16), V((3, T, W), BF16), V((T, E), BF16),
             V((2, NM, MR, HD), F32), V((2, NM, MR, HD), F32), V((NEP, EL // 2, MR, HD), BF16), V((NEP, EL // 2, MR, HD), BF16),
-            V((2, 2, NC, CR, HD), BF16), V((2, 8, T), F32), V((2, 8, TL), F32), V((T, 1), F32), V((T, 1), F32), V((T, E), F32), V((2, TL, HD), F32),
+            V((2, 2, NC, CR, HD), BF16), V((2, 8, T), F32), V((2, 8, TL), F32), V((T, 1), F32), V((T, 1), F32), V((T, E), F32), V((2, TL, HD), F32), V((2, EL * CAP, W), F32),
             dma((2,)), dma((3, EL)), dma((3,)), dma((3,)), dma((3,)), dma((2, 3)), dma((2, 3)), dma((2, NM)), dma((2, NM)),
             dma((2, EL // 2, 3)), dma((2, EL // 2, 3)), dma((2, 2, NC)), dma((2, 2, NC)), dma((3,)), dma((2,)), dma((1,)), dma((1,)), dma((7 + 4 * NC,)),
         ]
@@ -537,21 +597,21 @@
             out_specs=[any_] * 9,
             scratch_shapes=scratch,
             compiler_params=pltpu.CompilerParams(collective_id=0, has_side_effects=True, vmem_limit_bytes=60 * 1024 * 1024),
-        )(x, dy, prim.reshape(1, TL), alt.reshape(1, TL), wr, eg, eu, ed, sg, su, sd)
-
-        gg, gu, gd = pl.pallas_call(
+        )(x, dy, prim.reshape(1, TL), alt.reshape(1, TL), wr.T, eg, eu, ed, sg, su, sd)
+
+        gg, gu, gd, g_sg, g_su, g_sd, g_r, y, dx = pl.pallas_call(
             grads_kernel,
             name="grads",
             grid=(EL,),
-            out_shape=[sds((EL, D, W), F32), sds((EL, D, W), F32), sds((EL, W, D), F32)],
-            in_specs=[pl.BlockSpec((CAP, D), lambda i: (i, 0)), pl.BlockSpec((CAP, D), lambda i: (i, 0)), pl.BlockSpec((3, CAP, W), lambda i: (0, i, 0))],
-            out_specs=[pl.BlockSpec((1, D, W), lambda i: (i, 0, 0)), pl.BlockSpec((1, D, W), lambda i: (i, 0, 0)), pl.BlockSpec((1, W, D), lambda i: (i, 0, 0))],
-            compiler_params=pltpu.CompilerParams(vmem_limit_bytes=40 * 1024 * 1024),
-        )(nr, ur, act)
-        g_sg = jnp.einsum("td,tf->df", n_a, sact[1], preferred_element_type=F32)
-        g_su = jnp.einsum("td,tf->df", n_a, sact[2], preferred_element_type=F32)
-        g_sd = jnp.einsum("tf,td->fd", sact[0], dy_a, preferred_element_type=F32)
-        g_r = jnp.einsum("td,te->de", n_a, dl, preferred_element_type=F32)
-        return y, dx, gg, gu, gd, g_sg, g_su, g_sd, g_r
+            out_shape=[
+                sds((EL, D, W), F32), sds((EL, D, W), F32), sds((EL, W, D), F32),
+                sds((D, W), F32), sds((D, W), F32), sds((W, D), F32), sds((E, D), F32), sds((TL, D), BF16), sds((TL, D), BF16),
+            ],
+            in_specs=[pl.BlockSpec((CAP, D), lambda i: (i, 0)), pl.BlockSpec((CAP, D), lambda i: (i, 0)), pl.BlockSpec((3, CAP, W), lambda i: (0, i, 0)), any_, any_, vmem, vmem, any_, any_],
+            out_specs=[pl.BlockSpec((1, D, W), lambda i: (i, 0, 0)), pl.BlockSpec((1, D, W), lambda i: (i, 0, 0)), pl.BlockSpec((1, W, D), lambda i: (i, 0, 0))] + [any_] * 6,
+            scratch_shapes=[V((T, D), BF16), V((T, D), BF16), V((2, TL, D), BF16), V((2, D, W), F32), V((W, D), F32), V((E, D), F32), dma((4,)), dma((6,))],
+            compiler_params=pltpu.CompilerParams(vmem_limit_bytes=60 * 1024 * 1024),
+        )(nr, ur, act, n_a, dy_a, sact, dl, y, dx)
+        return y, dx, gg, gu, gd, g_sg, g_su, g_sd, g_r.T
 
     return jax.shard_map(step, mesh=mesh, in_specs=in_specs, out_specs=out_specs, check_vma=False)

time: 154 us -> 108 us (0.70)
  Pallas kernels: 143 us -> 107 us
  matrix products: 6.92 us -> 0 us
  local copies, waits for them, and re-layouts: 3.59 us -> 0 us
    pallas_call x1, Pallas kernels: 133 us -> 92.6 us  [step(): pl.pallas_call(line_kernel, name='line', out_shape=outs, in_specs=[any_,...]
    dot_general x4 -> x0, matrix products: 6.92 us -> none  [the longest x1 2.65 us: step(): g_r = jnp.einsum('td,te->de', n_a, dl, preferred_element_type=F32)]
    pallas_call x1, Pallas kernels: 9.67 us -> 14.3 us  [step(): pl.pallas_call(grads_kernel, name='grads', grid=(EL,), out_shape=[sds((EL...]
    unnamed x19 -> x0, local copies, waits for them, and re-layouts: 3.59 us -> none
where the time goes in v2:
time: 108 us
  Pallas kernels  107 us (99%)
    pallas_call x1, Pallas kernels, step(): pl.pallas_call(line_kernel, name='line', out_shape=outs, in_specs=[any_,...  92.6 us
    pallas_call x1, Pallas kernels, step(): pl.pallas_call(grads_kernel, name='grads', grid=(EL,), out_shape=[sds((EL...  14.3 us

profile of v2, /device:TPU:0, one launch (start us, length us, event | category | flops | bytes accessed | tf_op | source)
XLA Modules:
  0.0 107.5 jit_solution(16652587539091756891)
XLA Ops:
  0.6 92.6 %line.1 = (bf16[128,1536]{1,0:T(8,128)(2,1)}, bf16[128,1536]{1,0:T(8,128)(2,1)}, bf16[512,1536]{1,0:T(8,128)(2,1)}, bf16[512,1536]{1,0:T(8,128)(2,1)}, bf16[160,...) custom-call(bf16[128,1536]{1,0:T(8,128)(2,1)} %x_h.1, ...), custom_call_target="tpu_custom_call" | custom-call | tf_op jit(solution)/shard_map/line/pallas_call | solution.py:592
  93.3 14.3 %grads.1 = (f32[10,1536,128]{2,1,0:T(8,128)}, f32[10,1536,128]{2,1,0:T(8,128)}, f32[10,128,1536]{2,1,0:T(8,128)}, f32[1536,128]{1,0:T(8,128)}, f32[1536,128]{1,0...) custom-call(bf16[160,1536]{1,0:T(8,128)(2,1)} %get-tuple-element.27., ...), custom_call_target="tpu_custom_call" | custom-call | tf_op jit(solution)/shard_map/grads/pallas_call | solution.py:602

commit v3 on v2

--- a/solution.py
+++ b/solution.py
@@ -20,8 +20,13 @@
 EL = 10
 CAP = 16
 W = 128
-NM = 18
 MR = 32
+NS = TL // MR
+PE = MR // CAP
+NP = EL // PE
+O0 = 2 * NS
+N0 = O0 + NP
+NM = N0 + NP
 NC = 4
 CR = TL // NC
 
@@ -51,9 +56,9 @@
 
 def line_kernel(
     x_h, dy_h, prim_v, alt_v, wr_v, wg_h, wu_h, wd_h, sg_h, su_h, sd_h,
-    y_o, dx_o, n_o, dyo_o, nr_o, ur_o, act_o, sact_o, dl_o,
-    x_a, dy_a, n_a, u_a, ids, wg, wu, wd, sg, su, sd, nr, ur, act, sact, dl,
-    part, recv, o_all, dn_all, yb, dgb, pjb, tgt_v, g_v, df_v, dnr_v, ab,
+    y_o, dx_o, nr_o, ur_o, act_o, gs_o, gsd_o, gr_o,
+    x_a, dy_a, n_a, u_a, ids, wg, wu, wd, sg, su, sd, nr, ur, act, sact, dl, gs, gsd, gr,
+    part, recv, o_all, dn_all, yb, dxb, dgb, pjb, tgt_v, g_v, df_v, dnr_v, ab,
     xl, wl, sl, ids_s, ids_r, xs, xr, zs, zr, es, er, ys, yr, dgs, dgr, pjs, pjr, outs,
 ):
     z = lax.axis_index("etp")
@@ -158,20 +163,25 @@
     _, n_own = norm(x_a[mine, :].astype(F32))
     h_s, da_s, db_s = shared_acts(n_own, dy_a[mine, :])
     s_part = dot(h_s, sd[...])
-    for k in range(4):
+    for k in range(NS):
         part[0, k] = s_part[k * MR : (k + 1) * MR, :HD]
         part[1, k] = s_part[k * MR : (k + 1) * MR, HD:]
     dns_part = dot_t(da_s, sg[...]) + dot_t(db_s, su[...])
-    for k in range(4):
-        part[0, 4 + k] = dns_part[k * MR : (k + 1) * MR, :HD]
-        part[1, 4 + k] = dns_part[k * MR : (k + 1) * MR, HD:]
-    for m in range(8):
+    for k in range(NS):
+        part[0, NS + k] = dns_part[k * MR : (k + 1) * MR, :HD]
+        part[1, NS + k] = dns_part[k * MR : (k + 1) * MR, HD:]
+    for m in range(O0):
         source_send(m)
 
-    forward(1, 0)
-    forward(1, 1)
-    forward(1, 2)
-    forward(2, 0)
+    def forwards(hop1, hop2):
+        n1, n2 = len(hop1), len(hop2)
+        for i in range(max(n1, n2)):
+            if i < n1:
+                forward(1, hop1[i])
+            if i < n2:
+                forward(2, hop2[i])
+
+    forwards(range(0, 3), range(0, 1))
 
     for c in ids_c:
         c.wait_recv()
@@ -186,8 +196,7 @@
         return 0
 
     lax.fori_loop(0, NEP, norm_body, 0)
-    forward(1, 3)
-    forward(2, 1)
+    forwards(range(3, 4), range(1, 2))
 
     logits = dot_t(n_a[...], wr_v[...])
     ex = jnp.exp(logits - jnp.max(logits, axis=1, keepdims=True))
@@ -222,14 +231,11 @@
         tgt_v[...] - base == lax.broadcasted_iota(jnp.int32, (T, EL * CAP), 1).astype(F32), 1.0, 0.0
     ).astype(BF16)
     nr[...] = tdot(pick, n_a[...]).astype(BF16)
-    forward(1, 4)
-    forward(2, 2)
-    forward(1, 5)
-    forward(2, 3)
-
-    def fwd_pair(k, _):
-        for half in range(2):
-            i = 2 * k + half
+    forwards(range(4, 6), range(2, 4))
+
+    def expert_forward(k, _):
+        for half in range(PE):
+            i = PE * k + half
             for w in range(3):
                 wload(w, i).wait()
             sl16 = pl.ds(pl.multiple_of(i * CAP, CAP), CAP)
@@ -242,16 +248,13 @@
             act[0, sl16, :] = h
             o = dot(h, wd[i])
             r16 = slice(half * CAP, (half + 1) * CAP)
-            part[0, 8 + k, r16, :] = o[:, :HD]
-            part[1, 8 + k, r16, :] = o[:, HD:]
-        source_send(8 + k)
-        return 0
-
-    lax.fori_loop(0, EL // 2, fwd_pair, 0)
-    forward(1, 6)
-    forward(2, 4)
-    forward(1, 7)
-    forward(2, 5)
+            part[0, O0 + k, r16, :] = o[:, :HD]
+            part[1, O0 + k, r16, :] = o[:, HD:]
+        source_send(O0 + k)
+        return 0
+
+    lax.fori_loop(0, NP, expert_forward, 0)
+    forwards(range(6, 8), range(4, 6))
 
     x_c[1][0].wait_recv()
     relays[1].start()
@@ -265,24 +268,24 @@
     lax.fori_loop(0, NEP, u_body, 0)
     ur[...] = tdot(pick, u_a[...]).astype(BF16)
 
-    def pair_body(k, _):
-        for half in range(2):
-            i = 2 * k + half
+    def expert_backward(k, _):
+        for half in range(PE):
+            i = PE * k + half
             sl16 = pl.ds(pl.multiple_of(i * CAP, CAP), CAP)
             da, db = glu_grads(dot_t(ur[sl16, :], wd[i]), ab[0, sl16, :], ab[1, sl16, :])
             act[1, sl16, :] = da
             act[2, sl16, :] = db
+            dn = dot_t(da, wg[i]) + dot_t(db, wu[i])
             r16 = slice(half * CAP, (half + 1) * CAP)
-            dn = dot_t(da, wg[i]) + dot_t(db, wu[i])
-            part[0, 13 + k, r16, :] = dn[:, :HD]
-            part[1, 13 + k, r16, :] = dn[:, HD:]
-        source_send(13 + k)
-        return 0
-
-    lax.fori_loop(0, EL // 2, pair_body, 0)
+            part[0, N0 + k, r16, :] = dn[:, :HD]
+            part[1, N0 + k, r16, :] = dn[:, HD:]
+        source_send(N0 + k)
+        forward(1, O0 + k)
+        forward(2, O0 - 2 + k)
+        return 0
+
+    lax.fori_loop(0, NP, expert_backward, 0)
     stores = [
-        pltpu.make_async_copy(n_a, n_o, outs.at[0]),
-        pltpu.make_async_copy(dy_a, dyo_o, outs.at[1]),
         pltpu.make_async_copy(nr, nr_o, outs.at[2]),
         pltpu.make_async_copy(ur, ur_o, outs.at[3]),
         pltpu.make_async_copy(act, act_o, outs.at[4]),
@@ -290,15 +293,6 @@
     for c in stores:
         c.start()
 
-    def fwd_body(m, _):
-        forward(1, m)
-        forward(2, m - 2)
-        return 0
-
-    lax.fori_loop(8, NM, fwd_body, 0)
-    forward(2, NM - 2)
-    forward(2, NM - 1)
-
     def sact_body(j, _):
         h, da, db = shared_acts(n_a[rows(j), :], dy_a[rows(j), :])
         sact[0, rows(j), :] = h
@@ -306,10 +300,42 @@
         sact[2, rows(j), :] = db
         return 0
 
-    lax.fori_loop(0, NEP, sact_body, 0)
-    st = pltpu.make_async_copy(sact, sact_o, outs.at[5])
-    st.start()
-    stores.append(st)
+    def shared_grads(c, _):
+        cols = pl.ds(pl.multiple_of(c * W, W), W)
+        n_c = n_a[:, cols]
+        gs[0, cols, :] = tdot(n_c, sact[1])
+        gs[1, cols, :] = tdot(n_c, sact[2])
+        gsd[:, cols] = tdot(sact[0], dy_a[:, cols])
+        return 0
+
+    def piece_a(k):
+        sact_body(2 * k, 0)
+        sact_body(2 * k + 1, 0)
+
+    def piece_b(k):
+        lax.fori_loop(4 * k - 8, 4 * k - 4, shared_grads, 0)
+
+    def message_loop(step):
+        def with_piece(piece):
+            def body(k, _):
+                step(k)
+                piece(k)
+                return 0
+
+            return body
+
+        lax.fori_loop(0, 2, with_piece(piece_a), 0)
+        lax.fori_loop(2, NP, with_piece(piece_b), 0)
+
+    @pl.when(is_mid)
+    def _():
+        def step(k):
+            forward(1, N0 + k)
+            forward(2, N0 - 2 + k)
+
+        message_loop(step)
+        forward(2, NM - 2)
+        forward(2, NM - 1)
 
     def exchange(t, k, p):
         buf = (o_all, dn_all)[t]
@@ -337,15 +363,15 @@
         return 0
 
     def end_take_o(k, _):
-        take(hs, 8 + k)
-        o_all[e, k] = part[hs, 8 + k].astype(BF16)
+        take(hs, O0 + k)
+        o_all[e, k] = part[hs, O0 + k].astype(BF16)
         for p in range(3):
             exchange(0, k, p).start()
         return 0
 
     def end_take_dn(k, _):
-        take(hs, 13 + k)
-        dn_all[e, k] = part[hs, 13 + k].astype(BF16)
+        take(hs, N0 + k)
+        dn_all[e, k] = part[hs, N0 + k].astype(BF16)
         for p in range(3):
             exchange(1, k, p).start()
         return 0
@@ -356,7 +382,7 @@
                 exchange(t, k, p).wait_recv()
             return 0
 
-        lax.fori_loop(0, EL // 2, body, 0)
+        lax.fori_loop(0, NP, body, 0)
 
     def relay_copy(t, h, c):
         return rcopy(yb.at[t, h, c], yb.at[t, h, c], ys.at[t, h, c], yr.at[t, h, c], {"etp": jnp.clip(z + 1 - 2 * h, 0, 3)})
@@ -367,8 +393,10 @@
 
     @pl.when(is_end)
     def _():
-        lax.fori_loop(0, 8, end_take, 0)
-        lax.fori_loop(0, EL // 2, end_take_o, 0)
+        lax.fori_loop(0, O0, end_take, 0)
+
+        message_loop(lambda k: end_take_o(k, 0))
+        lax.fori_loop(0, 2, end_take_dn, 0)
         wait_exchange(0)
         o_flat = o_all[...].reshape(E * CAP, HD)
         for j in range(NEP):
@@ -378,11 +406,17 @@
         for k in range(3):
             dg_copy(hs, k).start()
         tok = dot(place(TL, pl.multiple_of(e * TL, TL)), o_flat)
-        s_own = part[hs, 0:4].reshape(TL, HD)
+        s_own = part[hs, 0:NS].reshape(TL, HD)
         y = (x_a[mine, lanes].astype(F32) + s_own + g_v[mine, :] * tok).astype(BF16)
         for c in range(NC):
             yb[0, hs, c] = y[c * CR : (c + 1) * CR, :]
         relay_start(0)
+        lax.fori_loop(2, NP, end_take_dn, 0)
+
+    late = [pltpu.make_async_copy(gs, gs_o, outs.at[0]), pltpu.make_async_copy(gsd, gsd_o, outs.at[1])]
+    for c in late:
+        c.start()
+    stores += late
 
     @pl.when(z != 0)
     def _():
@@ -397,9 +431,8 @@
         dg_col = jnp.transpose(jnp.broadcast_to(row, (TL, TL)))[:, 0:1]
         sl_j = slice(j * TL, (j + 1) * TL)
         dl[sl_j, :] = (dg_col * g_v[sl_j, :] * df_v[sl_j, :]).astype(BF16)
-    st = pltpu.make_async_copy(dl, dl_o, outs.at[6])
-    st.start()
-    stores.append(st)
+    def router_grad():
+        gr[...] = tdot(dl[...], n_a[...])
 
     def relay_wait(t, h, c):
         relay_copy(t, h, c).wait_recv()
@@ -425,6 +458,7 @@
 
     @pl.when(is_mid)
     def _():
+        router_grad()
         relay_through(0)
 
     @pl.when(is_end)
@@ -432,10 +466,10 @@
         dn_r = dot(dl[mine, :], wr_v[...])
         dnr_v[0] = dn_r[:, :HD]
         dnr_v[1] = dn_r[:, HD:]
-        lax.fori_loop(0, EL // 2, end_take_dn, 0)
+        router_grad()
         wait_exchange(1)
         tok = dot(place(TL, pl.multiple_of(e * TL, TL)), dn_all[...].reshape(E * CAP, HD))
-        dn = part[hs, 4:8].reshape(TL, HD) + dnr_v[hs] + tok
+        dn = part[hs, NS:O0].reshape(TL, HD) + dnr_v[hs] + tok
         dnr_v[hs] = dn
         xh = x_a[mine, lanes].astype(F32)
         pjb[hs, 0:1, :] = col_to_row(jnp.sum(dn * xh, axis=1, keepdims=True))
@@ -445,13 +479,19 @@
         row = pjb[0, 0:1, :] + pjb[1, 0:1, :]
         proj = jnp.transpose(jnp.broadcast_to(row, (TL, TL)))[:, 0:1] * (1.0 / D)
         dx = (dy_a[mine, lanes].astype(F32) + inv * dnr_v[hs] - x_a[mine, lanes].astype(F32) * (inv * inv * inv) * proj).astype(BF16)
-        for c in range(NC):
-            yb[1, hs, c] = dx[c * CR : (c + 1) * CR, :]
-        relay_start(1)
+        dxb[...] = dx
 
     @pl.when(is_end)
     def _():
         relay_through(0)
+
+    @pl.when(is_mid)
+    def _():
+        dxb[...] = jnp.zeros_like(dxb)
+
+    st = pltpu.make_async_copy(gr, gr_o, outs.at[5])
+    st.start()
+    stores.append(st)
 
     def out_copies(t, out):
         cs = []
@@ -464,11 +504,9 @@
     for c in oc:
         c.start()
     stores += oc
-    relay_through(1)
-    oc = out_copies(1, dx_o)
-    for c in oc:
-        c.start()
-    stores += oc
+    st = pltpu.make_async_copy(dxb, dx_o, outs.at[6])
+    st.start()
+    stores.append(st)
 
     for c in ids_c:
         c.wait_send()
@@ -498,12 +536,12 @@
                     exchange(t, k, p).wait_send()
             return 0
 
-        lax.fori_loop(0, EL // 2, drain, 0)
+        lax.fori_loop(0, NP, drain, 0)
         for k in range(3):
             dg_copy(hs, k).wait_send()
         pj_copy().wait_send()
 
-    for t in range(2):
+    for t in range(1):
         for c in range(NC):
             @pl.when(z != 3)
             def _(t=t, c=c):
@@ -517,49 +555,46 @@
         c.wait()
 
 
-def grads_kernel(nr, ur, act, n_h, dy_h, sact, dl, y_h, dx_h, gg, gu, gd, gsg_h, gsu_h, gsd_h, gr_h, yo_h, dxo_h, n, dy, yx, gs, gsd, gr, li, so):
-    i = pl.program_id(0)
-    loads = [pltpu.make_async_copy(a, b, li.at[k]) for k, (a, b) in enumerate(((n_h, n), (dy_h, dy), (y_h, yx.at[0]), (dx_h, yx.at[1])))]
-    pairs = ((gs.at[0], gsg_h), (gs.at[1], gsu_h), (gsd, gsd_h), (gr, gr_h), (yx.at[0], yo_h), (yx.at[1], dxo_h))
-    stores = [pltpu.make_async_copy(a, b, so.at[k]) for k, (a, b) in enumerate(pairs)]
-
-    @pl.when(i == 0)
-    def _():
-        for c in loads:
-            c.start()
-
-    @pl.when(i == 2)
-    def _():
-        for c in loads:
-            c.wait()
-        for c in stores[4:]:
-            c.start()
-        gs[0] = tdot(n[...], sact[1])
-        stores[0].start()
-
-    @pl.when(i == 3)
-    def _():
-        gs[1] = tdot(n[...], sact[2])
-        stores[1].start()
-
-    @pl.when(i == 4)
-    def _():
-        gsd[...] = tdot(sact[0], dy[...])
-        stores[2].start()
-
-    @pl.when(i == 5)
-    def _():
-        gr[...] = tdot(dl[...], n[...])
-        stores[3].start()
-
-    @pl.when(i == EL - 1)
-    def _():
-        for c in stores:
-            c.wait()
-
-    gg[0] = tdot(nr[...], act[1])
-    gu[0] = tdot(nr[...], act[2])
-    gd[0] = tdot(act[0], ur[...])
+def grads_kernel(nr_h, ur_h, act_h, gs_h, gsd_h, gr_h, y_h, gg_o, gu_o, gd_o, gsg_o, gsu_o, gsd_o, gr_o, y_o, nr, ur, act, gs, gsd, gr, yv, gg, gu, gd, ri, ro, li, so):
+    first = [pltpu.make_async_copy(a, b, ri.at[k]) for k, (a, b) in enumerate(((nr_h, nr), (ur_h, ur), (act_h, act)))]
+    through = ((gs_h.at[0], gs.at[0], gsg_o), (gs_h.at[1], gs.at[1], gsu_o), (gsd_h, gsd, gsd_o), (gr_h, gr, gr_o), (y_h, yv, y_o))
+    loads = [pltpu.make_async_copy(a, b, li.at[k]) for k, (a, b, _) in enumerate(through)]
+    stores = [pltpu.make_async_copy(b, c, so.at[k]) for k, (_, b, c) in enumerate(through)]
+    for c in first:
+        c.start()
+    for c in loads:
+        c.start()
+    for c in first:
+        c.wait()
+
+    def out(k, i):
+        src, dst = ((gg, gg_o), (gu, gu_o), (gd, gd_o))[k]
+        return pltpu.make_async_copy(src.at[i], dst.at[i], ro.at[k, i])
+
+    def body(i, _):
+        r = pl.ds(pl.multiple_of(i * CAP, CAP), CAP)
+        n = nr[r, :]
+        gg[i] = tdot(n, act[1, r, :])
+        out(0, i).start()
+        gu[i] = tdot(n, act[2, r, :])
+        out(1, i).start()
+        gd[i] = tdot(act[0, r, :], ur[r, :])
+        out(2, i).start()
+        return 0
+
+    lax.fori_loop(0, EL, body, 0)
+    for a, b in zip(loads, stores):
+        a.wait()
+        b.start()
+    for c in stores:
+        c.wait()
+
+    def drain(i, _):
+        for k in range(3):
+            out(k, i).wait()
+        return 0
+
+    lax.fori_loop(0, EL, drain, 0)
 
 
 def solution(mesh):
@@ -576,42 +611,52 @@
 
     def step(x, dy, prim, alt, wr, eg, eu, ed, sg, su, sd):
         outs = [
-            sds((TL, D), BF16), sds((TL, D), BF16), sds((T, D), BF16), sds((T, D), BF16),
-            sds((EL * CAP, D), BF16), sds((EL * CAP, D), BF16), sds((3, EL * CAP, W), BF16), sds((3, T, W), BF16), sds((T, E), BF16),
+            sds((TL, D), BF16), sds((TL, HD), BF16), sds((EL * CAP, D), BF16), sds((EL * CAP, D), BF16), sds((3, EL * CAP, W), BF16),
+            sds((2, D, W), F32), sds((W, D), F32), sds((E, D), F32),
         ]
         V = pltpu.VMEM
         scratch = [
             V((T, D), BF16), V((T, D), BF16), V((T, D), BF16), V((T, D), BF16), V((NEP, 8, TL), F32),
             V((EL, D, W), BF16), V((EL, D, W), BF16), V((EL, W, D), BF16), V((D, W), BF16), V((D, W), BF16), V((W, D), BF16),
-            V((EL * CAP, D), BF16), V((EL * CAP, D), BF16), V((3, EL * CAP, W), BF16), V((3, T, W), BF16), V((T, E), BF16),
-            V((2, NM, MR, HD), F32), V((2, NM, MR, HD), F32), V((NEP, EL // 2, MR, HD), BF16), V((NEP, EL // 2, MR, HD), BF16),
-            V((2, 2, NC, CR, HD), BF16), V((2, 8, T), F32), V((2, 8, TL), F32), V((T, 1), F32), V((T, 1), F32), V((T, E), F32), V((2, TL, HD), F32), V((2, EL * CAP, W), F32),
+            V((EL * CAP, D), BF16), V((EL * CAP, D), BF16), V((3, EL * CAP, W), BF16), V((3, T, W), BF16), V((T, E), BF16), V((2, D, W), F32), V((W, D), F32), V((E, D), F32),
+            V((2, NM, MR, HD), F32), V((2, NM, MR, HD), F32), V((NEP, NP, MR, HD), BF16), V((NEP, NP, MR, HD), BF16),
+            V((1, 2, NC, CR, HD), BF16), V((TL, HD), BF16), V((2, 8, T), F32), V((2, 8, TL), F32), V((T, 1), F32), V((T, 1), F32), V((T, E), F32), V((2, TL, HD), F32), V((2, EL * CAP, W), F32),
             dma((2,)), dma((3, EL)), dma((3,)), dma((3,)), dma((3,)), dma((2, 3)), dma((2, 3)), dma((2, NM)), dma((2, NM)),
-            dma((2, EL // 2, 3)), dma((2, EL // 2, 3)), dma((2, 2, NC)), dma((2, 2, NC)), dma((3,)), dma((2,)), dma((1,)), dma((1,)), dma((7 + 4 * NC,)),
+            dma((2, NP, 3)), dma((2, NP, 3)), dma((1, 2, NC)), dma((1, 2, NC)), dma((3,)), dma((2,)), dma((1,)), dma((1,)), dma((7 + 4 * NC,)),
         ]
-        y, dx, n_a, dy_a, nr, ur, act, sact, dl = pl.pallas_call(
+        y, dxh, nr, ur, act, gs, gsd, gr = pl.pallas_call(
             line_kernel,
             name="line",
             out_shape=outs,
             in_specs=[any_, any_, vmem, vmem, vmem] + [any_] * 6,
-            out_specs=[any_] * 9,
+            out_specs=[any_] * 8,
             scratch_shapes=scratch,
             compiler_params=pltpu.CompilerParams(collective_id=0, has_side_effects=True, vmem_limit_bytes=60 * 1024 * 1024),
         )(x, dy, prim.reshape(1, TL), alt.reshape(1, TL), wr.T, eg, eu, ed, sg, su, sd)
 
-        gg, gu, gd, g_sg, g_su, g_sd, g_r, y, dx = pl.pallas_call(
+        across = lax.ppermute(dxh, "etp", [(0, 3), (3, 0)])
+        far = lax.ppermute(dxh, "etp", [(0, 2), (3, 1)])
+        near = lax.ppermute(dxh, "etp", [(0, 1), (3, 2)])
+        gg, gu, gd, g_sg, g_su, g_sd, g_r, y = pl.pallas_call(
             grads_kernel,
             name="grads",
-            grid=(EL,),
             out_shape=[
                 sds((EL, D, W), F32), sds((EL, D, W), F32), sds((EL, W, D), F32),
-                sds((D, W), F32), sds((D, W), F32), sds((W, D), F32), sds((E, D), F32), sds((TL, D), BF16), sds((TL, D), BF16),
+                sds((D, W), F32), sds((D, W), F32), sds((W, D), F32), sds((E, D), F32), sds((TL, D), BF16),
             ],
-            in_specs=[pl.BlockSpec((CAP, D), lambda i: (i, 0)), pl.BlockSpec((CAP, D), lambda i: (i, 0)), pl.BlockSpec((3, CAP, W), lambda i: (0, i, 0)), any_, any_, vmem, vmem, any_, any_],
-            out_specs=[pl.BlockSpec((1, D, W), lambda i: (i, 0, 0)), pl.BlockSpec((1, D, W), lambda i: (i, 0, 0)), pl.BlockSpec((1, W, D), lambda i: (i, 0, 0))] + [any_] * 6,
-            scratch_shapes=[V((T, D), BF16), V((T, D), BF16), V((2, TL, D), BF16), V((2, D, W), F32), V((W, D), F32), V((E, D), F32), dma((4,)), dma((6,))],
+            in_specs=[any_] * 7,
+            out_specs=[any_] * 8,
+            scratch_shapes=[
+                V((EL * CAP, D), BF16), V((EL * CAP, D), BF16), V((3, EL * CAP, W), BF16), V((2, D, W), F32), V((W, D), F32), V((E, D), F32), V((TL, D), BF16),
+                V((EL, D, W), F32), V((EL, D, W), F32), V((EL, W, D), F32), dma((3,)), dma((3, EL)), dma((5,)), dma((5,)),
+            ],
+            cost_estimate=pl.CostEstimate(flops=30_000_000_000, bytes_accessed=32_000_000, transcendentals=0),
             compiler_params=pltpu.CompilerParams(vmem_limit_bytes=60 * 1024 * 1024),
-        )(nr, ur, act, n_a, dy_a, sact, dl, y, dx)
+        )(nr, ur, act, gs, gsd, gr, y)
+        z = lax.axis_index("etp")
+        left = jnp.where(z == 0, dxh, jnp.where(z == 1, near, jnp.where(z == 2, far, across)))
+        right = jnp.where(z == 3, dxh, jnp.where(z == 2, near, jnp.where(z == 1, far, across)))
+        dx = jnp.concatenate([left, right], axis=1)
         return y, dx, gg, gu, gd, g_sg, g_su, g_sd, g_r.T
 
     return jax.shard_map(step, mesh=mesh, in_specs=in_specs, out_specs=out_specs, check_vma=False)

time: 108 us -> 90.8 us (0.84)
  Pallas kernels: 107 us -> 82.3 us
  starting transfers between devices: 0 us -> 6.73 us
    pallas_call x1, Pallas kernels: 92.6 us -> 70.6 us  [step(): pl.pallas_call(line_kernel, name='line', out_shape=outs, in_specs=[any_,...]
    ppermute x0 -> x3, starting transfers between devices: none -> 6.73 us  [the longest x1 3.98 us: step(): across = lax.ppermute(dxh, 'etp', [(0, 3), (3, 0)])]
    pallas_call x1, Pallas kernels: 14.3 us -> 11.6 us  [step(): pl.pallas_call(grads_kernel, name='grads', out_shape=[sds((EL, D, W), F32...]
  transfers between devices with their start and end apart: 0 -> 3, of which waited for: 0 -> 0; matrix products, arithmetic and copies ran while one was open for 0% -> 0% of each run, Pallas kernels for 0% -> 13%
where the time goes in v3:
time: 90.8 us; the launch traced here: 90.6 us
  Pallas kernels  82.3 us (91%)
  starting transfers between devices  6.73 us (7%)
    pallas_call x1, Pallas kernels, step(): pl.pallas_call(line_kernel, name='line', out_shape=outs, in_specs=[any_,...  70.6 us
    pallas_call x1, Pallas kernels, step(): pl.pallas_call(grads_kernel, name='grads', out_shape=[sds((EL, D, W), F32...  11.6 us
    ppermute x1, starting transfers between devices, step(): across = lax.ppermute(dxh, 'etp', [(0, 3), (3, 0)])  3.98 us
  transfers between devices with their start and end apart: 3, of which 0 were waited for; matrix products, arithmetic and copies ran while one was open for 0% of the time, Pallas kernels for 13%

profile of v3, /device:TPU:0, one launch (start us, length us, event | category | flops | bytes accessed | tf_op | source)
XLA Modules:
  0.0 90.6 jit_solution(8017323742974229250)
XLA Ops:
  0.6 70.6 %line.1 = (bf16[128,1536]{1,0:T(8,128)(2,1)}, bf16[128,768]{1,0:T(8,128)(2,1)}, bf16[160,1536]{1,0:T(8,128)(2,1)}, bf16[160,1536]{1,0:T(8,128)(2,1)}, bf16[3,160...) custom-call(bf16[128,1536]{1,0:T(8,128)(2,1)} %x_h.1, ...), custom_call_target="tpu_custom_call" | custom-call | tf_op jit(solution)/shard_map/line/pallas_call | solution.py:627
  71.3 1.3 %collective-permute-start = (bf16[128,768]{1,0:T(8,128)(2,1)}, bf16[128,768]{1,0:T(8,128)(2,1)S(1)}, u32[]{:S(2)}, u32[]{:S(2)}) collective-permute-start(bf16[128,768]{1,0:T(8,128)(2,1)} %get-tuple-element.33), channel_id=1, source_target_pairs={{0,4},{12,8},{1,5},{13,9},{2,6},{14,10},{3,7},{15,11},{16,20},{28,... | collective-permute-start | bytes 589832 | tf_op jit(solution)/shard_map/ppermute | solution.py:639
  72.6 1.5 %collective-permute-start.1 = (bf16[128,768]{1,0:T(8,128)(2,1)}, bf16[128,768]{1,0:T(8,128)(2,1)S(1)}, u32[]{:S(2)}, u32[]{:S(2)}) collective-permute-start(bf16[128,768]{1,0:T(8,128)(2,1)} %get-tuple-element.33), channel_id=1, source_target_pairs={{0,8},{12,4},{1,9},{13,5},{2,10},{14,6},{3,11},{15,7},{16,24},{28,... | collective-permute-start | bytes 589832 | tf_op jit(solution)/shard_map/ppermute | solution.py:638
  74.1 4.0 %collective-permute-start.2 = (bf16[128,768]{1,0:T(8,128)(2,1)}, bf16[128,768]{1,0:T(8,128)(2,1)S(1)}, u32[]{:S(2)}, u32[]{:S(2)}) collective-permute-start(bf16[128,768]{1,0:T(8,128)(2,1)} %get-tuple-element.33), channel_id=1, source_target_pairs={{0,12},{12,0},{1,13},{13,1},{2,14},{14,2},{3,15},{15,3},{16,28},{2... | collective-permute-start | bytes 589832 | tf_op jit(solution)/shard_map/ppermute | solution.py:637
  78.0 0.0 copy-start
  78.1 11.6 %grads.1 = (f32[10,1536,128]{2,1,0:T(8,128)}, f32[10,1536,128]{2,1,0:T(8,128)}, f32[10,128,1536]{2,1,0:T(8,128)}, f32[1536,128]{1,0:T(8,128)}, f32[1536,128]{1,0...) custom-call(bf16[160,1536]{1,0:T(8,128)(2,1)} %get-tuple-element.25.nr_h, ...), custom_call_target="tpu_custom_call" | custom-call | flops 30000001024 | bytes 32000000 | tf_op jit(solution)/shard_map/grads/pallas_call | solution.py:640
  89.7 0.0 collective-permute-done
  89.7 0.0 collective-permute-done.1
  89.7 0.0 collective-permute-done.2
  89.7 0.0 copy-done
  89.8 0.8 pad_maximum_fusion
  (1 shorter events, 0.0 us)
Async XLA Ops:
  71.3 18.4 %collective-permute-start = (bf16[128,768]{1,0:T(8,128)(2,1)}, bf16[128,768]{1,0:T(8,128)(2,1)S(1)}, u32[]{:S(2)}, u32[]{:S(2)}) collective-permute-start(bf16[128,768]{1,0:T(8,128)(2,1)} %get-tuple-element.33), channel_id=1, source_target_pairs={{0,4},{12,8},{1,5},{13,9},{2,6},{14,10},{3,7},{15,11},{16,20},{28,... | collective-permute-start | bytes 589832 | tf_op jit(solution)/shard_map/ppermute | solution.py:639
  72.6 17.1 %collective-permute-start.1 = (bf16[128,768]{1,0:T(8,128)(2,1)}, bf16[128,768]{1,0:T(8,128)(2,1)S(1)}, u32[]{:S(2)}, u32[]{:S(2)}) collective-permute-start(bf16[128,768]{1,0:T(8,128)(2,1)} %get-tuple-element.33), channel_id=1, source_target_pairs={{0,8},{12,4},{1,9},{13,5},{2,10},{14,6},{3,11},{15,7},{16,24},{28,... | collective-permute-start | bytes 589832 | tf_op jit(solution)/shard_map/ppermute | solution.py:638
  74.1 15.7 %collective-permute-start.2 = (bf16[128,768]{1,0:T(8,128)(2,1)}, bf16[128,768]{1,0:T(8,128)(2,1)S(1)}, u32[]{:S(2)}, u32[]{:S(2)}) collective-permute-start(bf16[128,768]{1,0:T(8,128)(2,1)} %get-tuple-element.33), channel_id=1, source_target_pairs={{0,12},{12,0},{1,13},{13,1},{2,14},{14,2},{3,15},{15,3},{16,28},{2... | collective-permute-start | bytes 589832 | tf_op jit(solution)/shard_map/ppermute | solution.py:637
  78.0 11.7 %copy-start = (bf16[128,768]{1,0:T(8,128)(2,1)S(1)}, bf16[128,768]{1,0:T(8,128)(2,1)}, u32[]{:S(2)}) copy-start(bf16[128,768]{1,0:T(8,128)(2,1)} %get-tuple-element.33) | copy-start | bytes 589828

commit v4 on v3

--- a/solution.py
+++ b/solution.py
@@ -1,11 +1,10 @@
-import functools
-
 import jax
 import jax.numpy as jnp
 from jax import lax
 from jax.experimental import pallas as pl
 from jax.experimental.pallas import tpu as pltpu
 from jax.sharding import PartitionSpec as P
+
 
 EPS = 1e-5
 F32 = jnp.float32
@@ -21,12 +20,13 @@
 CAP = 16
 W = 128
 MR = 32
-NS = TL // MR
+FB = 32 // MR
 PE = MR // CAP
 NP = EL // PE
-O0 = 2 * NS
+O0 = 0
 N0 = O0 + NP
 NM = N0 + NP
+PR = D // 8
 NC = 4
 CR = TL // NC
 
@@ -57,12 +57,13 @@
 def line_kernel(
     x_h, dy_h, prim_v, alt_v, wr_v, wg_h, wu_h, wd_h, sg_h, su_h, sd_h,
     y_o, dx_o, nr_o, ur_o, act_o, gs_o, gsd_o, gr_o,
-    x_a, dy_a, n_a, u_a, ids, wg, wu, wd, sg, su, sd, nr, ur, act, sact, dl, gs, gsd, gr,
-    part, recv, o_all, dn_all, yb, dxb, dgb, pjb, tgt_v, g_v, df_v, dnr_v, ab,
-    xl, wl, sl, ids_s, ids_r, xs, xr, zs, zr, es, er, ys, yr, dgs, dgr, pjs, pjr, outs,
+    x_a, dy_a, n_a, u_a, ids, wg, wu, wd, wsh, sd, s_v, ds_v, nr, ur, act, sact, dl, gs, gsd, gr,
+    part, recv, o_all, dn_all, yb, dxb, dgb, pjb, qb, xrow, tgt_v, g_v, df_v, dnr_v, ab,
+    xl, wl, sl, ids_s, ids_r, xs, xr, zs, zr, es, er, ys, yr, dgs, dgr, pjs, pjr, w1s, w1r, w2s, w2r, qs, qr, outs,
 ):
     z = lax.axis_index("etp")
     e = lax.axis_index("ep")
+    dp = lax.axis_index("dp")
     e_y, e_c, e_d = e ^ 2, e ^ 1, e ^ 3
     peers = (e_y, e_c, e_d)
     is_end = (z == 0) | (z == 3)
@@ -77,7 +78,7 @@
     ldy = pltpu.make_async_copy(dy_h, dy_a.at[mine], xl.at[1])
     lx.start()
     ldy.start()
-    shared_loads = [pltpu.make_async_copy(a, b, sl.at[k]) for k, (a, b) in enumerate(((sg_h, sg), (su_h, su), (sd_h, sd)))]
+    shared_loads = [pltpu.make_async_copy(a, b, sl.at[k]) for k, (a, b) in enumerate(((sg_h, wsh.at[z, 0]), (su_h, wsh.at[z, 1]), (sd_h, sd)))]
     for c in shared_loads:
         c.start()
 
@@ -94,7 +95,13 @@
         pl.semaphore_signal(barrier, inc=1, device_id={"ep": q}, device_id_type=MESH)
     for k in range(1, 4):
         pl.semaphore_signal(barrier, inc=1, device_id={"etp": lax.rem(z + k, 4)}, device_id_type=MESH)
-    pl.semaphore_wait(barrier, 6)
+    pl.semaphore_signal(barrier, inc=1, device_id={"dp": 1 - dp}, device_id_type=MESH)
+    for q in peers:
+        pl.semaphore_signal(barrier, inc=1, device_id={"etp": 3 - z, "ep": q}, device_id_type=MESH)
+    for c in shared_loads:
+        c.wait()
+    wsh[z, 2] = sd[...].T
+    pl.semaphore_wait(barrier, 10)
 
     def rcopy(src, dst, s, r, dev):
         return pltpu.make_async_remote_copy(src_ref=src, dst_ref=dst, send_sem=s, recv_sem=r, device_id=dev, device_id_type=MESH)
@@ -150,57 +157,46 @@
         inv = lax.rsqrt(jnp.mean(xw * xw, axis=1, keepdims=True) + EPS)
         return inv, (xw * inv).astype(BF16)
 
-    for c in shared_loads:
-        c.wait()
-
-    def shared_acts(n, dy):
-        a = dot(n, sg[...])
-        b = dot(n, su[...])
+    def shared_acts(n, dy, j):
+        a = dot(n, wsh[j, 0])
+        b = dot(n, wsh[j, 1])
         h = glu(a, b)
-        dg_, du_ = glu_grads(dot_t(dy, sd[...]), a, b)
+        dg_, du_ = glu_grads(dot(dy, wsh[j, 2]), a, b)
         return h, dg_, du_
 
-    _, n_own = norm(x_a[mine, :].astype(F32))
-    h_s, da_s, db_s = shared_acts(n_own, dy_a[mine, :])
-    s_part = dot(h_s, sd[...])
-    for k in range(NS):
-        part[0, k] = s_part[k * MR : (k + 1) * MR, :HD]
-        part[1, k] = s_part[k * MR : (k + 1) * MR, HD:]
-    dns_part = dot_t(da_s, sg[...]) + dot_t(db_s, su[...])
-    for k in range(NS):
-        part[0, NS + k] = dns_part[k * MR : (k + 1) * MR, :HD]
-        part[1, NS + k] = dns_part[k * MR : (k + 1) * MR, HD:]
-    for m in range(O0):
-        source_send(m)
-
-    def forwards(hop1, hop2):
-        n1, n2 = len(hop1), len(hop2)
-        for i in range(max(n1, n2)):
-            if i < n1:
-                forward(1, hop1[i])
-            if i < n2:
-                forward(2, hop2[i])
-
-    forwards(range(0, 3), range(0, 1))
+    def piece(dp_, e_):
+        return pl.ds(pl.multiple_of((dp_ * NEP + e_) * PR, 64), PR)
+
+    def to_end(j, end):
+        ref = wsh.at[j, :, piece(dp, e)]
+        return rcopy(ref, ref, w1s.at[end // 3], w1r.at[j], {"etp": end})
+
+    for end in (0, 3):
+        @pl.when(z != end)
+        def _(end=end):
+            to_end(z, end).start()
+
+    foreign = pl.ds(1 - hs, 3)
+
+    def w_swap(k, dp_, e_, target, part_of=None):
+        span = piece(dp_, e_)
+        if part_of is not None:
+            span = pl.ds(pl.multiple_of((dp_ * NEP + e_) * PR + part_of * (PR // 2), 32), PR // 2)
+        ref = wsh.at[foreign, :, span]
+        return rcopy(ref, ref, w2s.at[k], w2r.at[k], target)
+
+    to_x, to_y, to_c = {"dp": 1 - dp}, {"ep": e_y}, {"ep": e_c}
+    w_send = [
+        w_swap(0, dp, e, to_x), w_swap(1, dp, e, to_y), w_swap(2, dp, e, to_c), w_swap(3, dp, e_y, to_x, 0),
+        w_swap(4, 1 - dp, e, to_c), w_swap(5, dp, e_y, to_c), w_swap(6, 1 - dp, e_y, to_c), w_swap(7, 1 - dp, e, to_y, 1),
+    ]
+    w_recv = [
+        w_swap(0, 1 - dp, e, to_x), w_swap(1, dp, e_y, to_y), w_swap(2, dp, e_c, to_c), w_swap(3, 1 - dp, e_y, to_x, 0),
+        w_swap(4, 1 - dp, e_c, to_c), w_swap(5, dp, e_d, to_c), w_swap(6, 1 - dp, e_d, to_c), w_swap(7, 1 - dp, e_y, to_y, 1),
+    ]
 
     for c in ids_c:
         c.wait_recv()
-    x_c[0][0].wait_recv()
-    relays[0].start()
-    x_c[0][1].wait_recv()
-    relays[0].wait_recv()
-
-    def norm_body(j, _):
-        _, n = norm(x_a[rows(j), :].astype(F32))
-        n_a[rows(j), :] = n
-        return 0
-
-    lax.fori_loop(0, NEP, norm_body, 0)
-    forwards(range(3, 4), range(1, 2))
-
-    logits = dot_t(n_a[...], wr_v[...])
-    ex = jnp.exp(logits - jnp.max(logits, axis=1, keepdims=True))
-    probs = ex / jnp.sum(ex, axis=1, keepdims=True)
     cols = []
     for j in range(NEP):
         block = jnp.concatenate([ids[j], jnp.zeros((TL - 8, TL), F32)], axis=0)
@@ -223,15 +219,26 @@
     eid = jnp.sum(one_s * iota_e, axis=1, keepdims=True)
     has = (1.0 - over) + keep_a
     tgt_v[...] = jnp.where(has > 0.5, eid * CAP + slot, -1.0)
-    g_v[...] = jnp.sum(probs * one_s, axis=1, keepdims=True)
-    df_v[...] = one_s - probs
+    df_v[...] = one_s
 
     base = (e * (EL * CAP)).astype(F32)
     pick = jnp.where(
         tgt_v[...] - base == lax.broadcasted_iota(jnp.int32, (T, EL * CAP), 1).astype(F32), 1.0, 0.0
     ).astype(BF16)
+
+    def norm_rows(j):
+        _, n = norm(x_a[rows(j), :].astype(F32))
+        n_a[rows(j), :] = n
+
+    norm_rows(e)
+    x_c[0][1].wait_recv()
+    norm_rows(e_c)
+    x_c[0][0].wait_recv()
+    relays[0].start()
+    norm_rows(e_y)
+    relays[0].wait_recv()
+    norm_rows(e_d)
     nr[...] = tdot(pick, n_a[...]).astype(BF16)
-    forwards(range(4, 6), range(2, 4))
 
     def expert_forward(k, _):
         for half in range(PE):
@@ -254,7 +261,21 @@
         return 0
 
     lax.fori_loop(0, NP, expert_forward, 0)
-    forwards(range(6, 8), range(4, 6))
+
+    @pl.when(is_end)
+    def _():
+        for k in range(3):
+            to_end(1 - hs + k, 0).wait_recv()
+        for k in range(3):
+            w_send[k].start()
+
+    logits = dot_t(n_a[...], wr_v[...])
+    ex = jnp.exp(logits - jnp.max(logits, axis=1, keepdims=True))
+    probs = ex / jnp.sum(ex, axis=1, keepdims=True)
+    g_v[...] = jnp.sum(probs * df_v[...], axis=1, keepdims=True)
+    df_v[...] = df_v[...] - probs
+    for m in range(2 * FB):
+        forward(1, m)
 
     x_c[1][0].wait_recv()
     relays[1].start()
@@ -267,6 +288,11 @@
 
     lax.fori_loop(0, NEP, u_body, 0)
     ur[...] = tdot(pick, u_a[...]).astype(BF16)
+
+    @pl.when(is_end)
+    def _():
+        xrow[...] = tdot(pick, x_a[...]).astype(BF16)
+
 
     def expert_backward(k, _):
         for half in range(PE):
@@ -280,8 +306,8 @@
             part[0, N0 + k, r16, :] = dn[:, :HD]
             part[1, N0 + k, r16, :] = dn[:, HD:]
         source_send(N0 + k)
-        forward(1, O0 + k)
-        forward(2, O0 - 2 + k)
+        forward(1, 2 * FB + k)
+        forward(2, k)
         return 0
 
     lax.fori_loop(0, NP, expert_backward, 0)
@@ -293,8 +319,8 @@
     for c in stores:
         c.start()
 
-    def sact_body(j, _):
-        h, da, db = shared_acts(n_a[rows(j), :], dy_a[rows(j), :])
+    def sact_body(j):
+        h, da, db = shared_acts(n_a[rows(j), :], dy_a[rows(j), :], z)
         sact[0, rows(j), :] = h
         sact[1, rows(j), :] = da
         sact[2, rows(j), :] = db
@@ -309,37 +335,31 @@
         return 0
 
     def piece_a(k):
-        sact_body(2 * k, 0)
-        sact_body(2 * k + 1, 0)
+        sact_body(2 * k)
+        sact_body(2 * k + 1)
 
     def piece_b(k):
         lax.fori_loop(4 * k - 8, 4 * k - 4, shared_grads, 0)
 
-    def message_loop(step):
-        def with_piece(piece):
-            def body(k, _):
-                step(k)
-                piece(k)
-                return 0
-
-            return body
-
-        lax.fori_loop(0, 2, with_piece(piece_a), 0)
-        lax.fori_loop(2, NP, with_piece(piece_b), 0)
-
     @pl.when(is_mid)
     def _():
-        def step(k):
-            forward(1, N0 + k)
-            forward(2, N0 - 2 + k)
-
-        message_loop(step)
-        forward(2, NM - 2)
-        forward(2, NM - 1)
+        for k in range(NP):
+            if k < NP - 2 * FB:
+                forward(1, NP + 2 * FB + k)
+            forward(2, NP + k)
+            if k % FB == FB - 1:
+                if k // FB < 2:
+                    piece_a(k // FB)
+                else:
+                    piece_b(k // FB)
 
     def exchange(t, k, p):
-        buf = (o_all, dn_all)[t]
-        return rcopy(buf.at[e, k], buf.at[e, k], es.at[t, k, p], er.at[t, k, p], {"ep": peers[p]})
+        ref = (o_all, dn_all)[t].at[e_y if p == 2 else e, k]
+        return rcopy(ref, ref, es.at[t, k, p], er.at[t, k, p], {"ep": e_y if p == 0 else e_c})
+
+    def pass_on(t, k):
+        exchange(t, k, 0).wait_recv()
+        exchange(t, k, 2).start()
 
     lanes = pl.ds(pl.multiple_of(hs * HD, 128), HD)
 
@@ -358,28 +378,47 @@
     def pj_copy():
         return rcopy(pjb.at[hs], pjb.at[hs], pjs.at[0], pjr.at[0], {"etp": 3 - z})
 
-    def end_take(m, _):
-        take(hs, m)
-        return 0
-
     def end_take_o(k, _):
         take(hs, O0 + k)
         o_all[e, k] = part[hs, O0 + k].astype(BF16)
-        for p in range(3):
+        for p in range(2):
             exchange(0, k, p).start()
-        return 0
+
+        @pl.when(k >= 2 * FB)
+        def _():
+            pass_on(0, k - 2 * FB)
+
+        return 0
+
+    def q_copy(r):
+        ref = qb.at[hs, e]
+        return rcopy(ref, ref, qs.at[r], qr.at[r], {"etp": 3 - z, "ep": e ^ r})
 
     def end_take_dn(k, _):
         take(hs, N0 + k)
-        dn_all[e, k] = part[hs, N0 + k].astype(BF16)
-        for p in range(3):
+        rounded = part[hs, N0 + k].astype(BF16)
+        dn_all[e, k] = rounded
+        for p in range(2):
             exchange(1, k, p).start()
+        q = jnp.sum(rounded.astype(F32) * xrow[pl.ds(pl.multiple_of(k * MR, MR), MR), lanes].astype(F32), axis=1, keepdims=True)
+        diag = lax.broadcasted_iota(jnp.int32, (MR, 128), 0) == lax.broadcasted_iota(jnp.int32, (MR, 128), 1)
+        q_row = jnp.sum(jnp.where(diag, q, 0.0), axis=0, keepdims=True)
+        at_k = lax.broadcasted_iota(jnp.int32, (16, 128), 0) == k
+        qb[hs, e] = jnp.where(at_k, q_row, jnp.where(k == 0, 0.0, qb[hs, e]))
+
+        @pl.when(k >= 2 * FB)
+        def _():
+            pass_on(1, k - 2 * FB)
+
         return 0
 
     def wait_exchange(t):
+        for k in range(NP - 2 * FB, NP):
+            pass_on(t, k)
+
         def body(k, _):
-            for p in range(3):
-                exchange(t, k, p).wait_recv()
+            exchange(t, k, 1).wait_recv()
+            exchange(t, k, 2).wait_recv()
             return 0
 
         lax.fori_loop(0, NP, body, 0)
@@ -393,44 +432,90 @@
 
     @pl.when(is_end)
     def _():
-        lax.fori_loop(0, O0, end_take, 0)
-
-        message_loop(lambda k: end_take_o(k, 0))
-        lax.fori_loop(0, 2, end_take_dn, 0)
+        w_recv[0].wait_recv()
+        w_send[4].start()
+        w_send[7].start()
+
+        def takes(fn, g, n=1):
+            lax.fori_loop(g * FB, (g + n) * FB, fn, 0)
+
+        takes(end_take_o, 0)
+        piece_a(0)
+        w_recv[1].wait_recv()
+        w_send[3].start()
+        w_send[5].start()
+        takes(end_take_o, 1)
+        piece_a(1)
+        takes(end_take_o, 2)
+        w_recv[3].wait_recv()
+        w_recv[7].wait_recv()
+        w_send[6].start()
+        takes(end_take_o, 3)
+        piece_b(2)
+        takes(end_take_o, 4)
+        for k in (2, 4, 5, 6):
+            w_recv[k].wait_recv()
+        half = pl.ds(pl.multiple_of(hs * HD, 128), HD)
+
+        def slice_body(j, _):
+            h, da, db = shared_acts(n_a[mine, :], dy_a[mine, :], j)
+            s_j = dot_t(h, wsh[j, 2, half, :])
+            ds_j = dot_t(da, wsh[j, 0, half, :]) + dot_t(db, wsh[j, 1, half, :])
+            s_v[...] += s_j
+            ds_v[...] += ds_j
+            return 0
+
+        s_v[...] = jnp.zeros_like(s_v)
+        ds_v[...] = jnp.zeros_like(ds_v)
+        lax.fori_loop(0, 4, slice_body, 0)
+        pjb[hs, 0:1, :] = col_to_row(jnp.sum(ds_v[...] * x_a[mine, lanes].astype(F32), axis=1, keepdims=True))
+        pj_copy().start()
+        takes(end_take_dn, 0)
         wait_exchange(0)
         o_flat = o_all[...].reshape(E * CAP, HD)
+        tok = dot(place(TL, pl.multiple_of(e * TL, TL)), o_flat)
+        y = (x_a[mine, lanes].astype(F32) + s_v[...] + g_v[mine, :] * tok).astype(BF16)
+        for c in range(NC):
+            yb[0, hs, c] = y[c * CR : (c + 1) * CR, :]
+        relay_start(0)
+        lane = lax.broadcasted_iota(jnp.int32, (TL, TL), 1)
+        packed = jnp.zeros((TL, TL), F32)
         for j in range(NEP):
             tok = dot(place(TL, j * TL), o_flat)
             prod = dy_a[j * TL : (j + 1) * TL, lanes].astype(F32) * tok
-            dgb[hs, 0:1, j * TL : (j + 1) * TL] = col_to_row(jnp.sum(prod, axis=1, keepdims=True))
+            packed = jnp.where(lane == j, jnp.sum(prod, axis=1, keepdims=True), packed)
+        dgb[hs] = jnp.transpose(packed)[0:8, :]
         for k in range(3):
             dg_copy(hs, k).start()
-        tok = dot(place(TL, pl.multiple_of(e * TL, TL)), o_flat)
-        s_own = part[hs, 0:NS].reshape(TL, HD)
-        y = (x_a[mine, lanes].astype(F32) + s_own + g_v[mine, :] * tok).astype(BF16)
-        for c in range(NC):
-            yb[0, hs, c] = y[c * CR : (c + 1) * CR, :]
-        relay_start(0)
-        lax.fori_loop(2, NP, end_take_dn, 0)
+        takes(end_take_dn, 1)
+        piece_b(3)
+        takes(end_take_dn, 2)
+        piece_b(4)
+        takes(end_take_dn, 3, 2)
+        for r in range(4):
+            q_copy(r).start()
 
     late = [pltpu.make_async_copy(gs, gs_o, outs.at[0]), pltpu.make_async_copy(gsd, gsd_o, outs.at[1])]
     for c in late:
         c.start()
     stores += late
 
-    @pl.when(z != 0)
-    def _():
-        dg_copy(0, 0).wait_recv()
-
-    @pl.when(z != 3)
-    def _():
-        dg_copy(1, 0).wait_recv()
-
-    for j in range(NEP):
-        row = dgb[0, 0:1, j * TL : (j + 1) * TL] + dgb[1, 0:1, j * TL : (j + 1) * TL]
-        dg_col = jnp.transpose(jnp.broadcast_to(row, (TL, TL)))[:, 0:1]
-        sl_j = slice(j * TL, (j + 1) * TL)
-        dl[sl_j, :] = (dg_col * g_v[sl_j, :] * df_v[sl_j, :]).astype(BF16)
+    def wait_dg():
+        @pl.when(z != 0)
+        def _():
+            dg_copy(0, 0).wait_recv()
+
+        @pl.when(z != 3)
+        def _():
+            dg_copy(1, 0).wait_recv()
+
+    def make_dl():
+        dg_rows = jnp.concatenate([dgb[0] + dgb[1], jnp.zeros((TL - 8, TL), F32)], axis=0)
+        dg_cols = jnp.transpose(dg_rows)
+        for j in range(NEP):
+            sl_j = slice(j * TL, (j + 1) * TL)
+            dl[sl_j, :] = (dg_cols[:, j : j + 1] * g_v[sl_j, :] * df_v[sl_j, :]).astype(BF16)
+
     def router_grad():
         gr[...] = tdot(dl[...], n_a[...])
 
@@ -458,26 +543,41 @@
 
     @pl.when(is_mid)
     def _():
+        relay_through(0)
+        wait_dg()
+        make_dl()
         router_grad()
-        relay_through(0)
 
     @pl.when(is_end)
     def _():
+        wait_dg()
+        make_dl()
         dn_r = dot(dl[mine, :], wr_v[...])
         dnr_v[0] = dn_r[:, :HD]
         dnr_v[1] = dn_r[:, HD:]
         router_grad()
         wait_exchange(1)
         tok = dot(place(TL, pl.multiple_of(e * TL, TL)), dn_all[...].reshape(E * CAP, HD))
-        dn = part[hs, NS:O0].reshape(TL, HD) + dnr_v[hs] + tok
-        dnr_v[hs] = dn
-        xh = x_a[mine, lanes].astype(F32)
-        pjb[hs, 0:1, :] = col_to_row(jnp.sum(dn * xh, axis=1, keepdims=True))
-        pj_copy().start()
+        dn = ds_v[...] + dnr_v[hs] + tok
+        other_lanes = pl.ds(pl.multiple_of((1 - hs) * HD, 128), HD)
+        own = jnp.sum(dn * x_a[mine, lanes].astype(F32), axis=1, keepdims=True)
+        rest = jnp.sum(dnr_v[1 - hs] * x_a[mine, other_lanes].astype(F32), axis=1, keepdims=True)
         inv, _ = norm(x_a[mine, :].astype(F32))
         pj_copy().wait_recv()
-        row = pjb[0, 0:1, :] + pjb[1, 0:1, :]
-        proj = jnp.transpose(jnp.broadcast_to(row, (TL, TL)))[:, 0:1] * (1.0 / D)
+        far_s = jnp.transpose(jnp.broadcast_to(pjb[1 - hs, 0:1, :], (TL, TL)))[:, 0:1]
+        dnr_v[hs] = dn
+        for r in range(4):
+            q_copy(r).wait_recv()
+        t_own = tgt_v[mine, :]
+        lane = lax.broadcasted_iota(jnp.int32, (TL, 128), 1).astype(F32)
+
+        def q_body(i, acc):
+            start = (i * MR).astype(F32)
+            hit = (t_own - start == lane) & (lane < MR)
+            return acc + jnp.where(hit, qb[1 - hs, i // NP, pl.ds(lax.rem(i, NP), 1), :], 0.0)
+
+        picked = lax.fori_loop(0, NEP * NP, q_body, jnp.zeros((TL, 128), F32))
+        proj = (own + rest + far_s + jnp.sum(picked, axis=1, keepdims=True)) * (1.0 / D)
         dx = (dy_a[mine, lanes].astype(F32) + inv * dnr_v[hs] - x_a[mine, lanes].astype(F32) * (inv * inv * inv) * proj).astype(BF16)
         dxb[...] = dx
 
@@ -515,6 +615,16 @@
             c.wait_send()
         relays[k].wait_send()
 
+    for end in (0, 3):
+        @pl.when(z != end)
+        def _(end=end):
+            to_end(z, end).wait_send()
+
+    @pl.when(is_end)
+    def _():
+        for c in w_send:
+            c.wait_send()
+
     def line_drain(m, _):
         @pl.when(z != 0)
         def _():
@@ -540,6 +650,8 @@
         for k in range(3):
             dg_copy(hs, k).wait_send()
         pj_copy().wait_send()
+        for r in range(4):
+            q_copy(r).wait_send()
 
     for t in range(1):
         for c in range(NC):
@@ -617,12 +729,12 @@
         V = pltpu.VMEM
         scratch = [
             V((T, D), BF16), V((T, D), BF16), V((T, D), BF16), V((T, D), BF16), V((NEP, 8, TL), F32),
-            V((EL, D, W), BF16), V((EL, D, W), BF16), V((EL, W, D), BF16), V((D, W), BF16), V((D, W), BF16), V((W, D), BF16),
+            V((EL, D, W), BF16), V((EL, D, W), BF16), V((EL, W, D), BF16), V((4, 3, D, W), BF16), V((W, D), BF16), V((TL, HD), F32), V((TL, HD), F32),
             V((EL * CAP, D), BF16), V((EL * CAP, D), BF16), V((3, EL * CAP, W), BF16), V((3, T, W), BF16), V((T, E), BF16), V((2, D, W), F32), V((W, D), F32), V((E, D), F32),
             V((2, NM, MR, HD), F32), V((2, NM, MR, HD), F32), V((NEP, NP, MR, HD), BF16), V((NEP, NP, MR, HD), BF16),
-            V((1, 2, NC, CR, HD), BF16), V((TL, HD), BF16), V((2, 8, T), F32), V((2, 8, TL), F32), V((T, 1), F32), V((T, 1), F32), V((T, E), F32), V((2, TL, HD), F32), V((2, EL * CAP, W), F32),
+            V((1, 2, NC, CR, HD), BF16), V((TL, HD), BF16), V((2, 8, TL), F32), V((2, 8, TL), F32), V((2, NEP, 16, 128), F32), V((EL * CAP, D), BF16), V((T, 1), F32), V((T, 1), F32), V((T, E), F32), V((2, TL, HD), F32), V((2, EL * CAP, W), F32),
             dma((2,)), dma((3, EL)), dma((3,)), dma((3,)), dma((3,)), dma((2, 3)), dma((2, 3)), dma((2, NM)), dma((2, NM)),
-            dma((2, NP, 3)), dma((2, NP, 3)), dma((1, 2, NC)), dma((1, 2, NC)), dma((3,)), dma((2,)), dma((1,)), dma((1,)), dma((7 + 4 * NC,)),
+            dma((2, NP, 3)), dma((2, NP, 3)), dma((1, 2, NC)), dma((1, 2, NC)), dma((3,)), dma((2,)), dma((1,)), dma((1,)), dma((2,)), dma((4,)), dma((8,)), dma((8,)), dma((4,)), dma((4,)), dma((7 + 4 * NC,)),
         ]
         y, dxh, nr, ur, act, gs, gsd, gr = pl.pallas_call(
             line_kernel,

time: 90.8 us -> 85.9 us (0.946)
  Pallas kernels: 82.3 us -> 77.8 us
    pallas_call x1, Pallas kernels: 70.6 us -> 66.2 us  [step(): pl.pallas_call(line_kernel, name='line', out_shape=outs, in_specs=[any_,...]
  transfers between devices with their start and end apart: 3 -> 3, of which waited for: 0 -> 0; matrix products, arithmetic and copies ran while one was open for 0% -> 0% of each run, Pallas kernels for 13% -> 14%
where the time goes in v4:
time: 85.9 us; the launch traced here: 85.6 us
  Pallas kernels  77.8 us (91%)
  starting transfers between devices  6.26 us (7%)
    pallas_call x1, Pallas kernels, step(): pl.pallas_call(line_kernel, name='line', out_shape=outs, in_specs=[any_,...  66.2 us
    pallas_call x1, Pallas kernels, step(): pl.pallas_call(grads_kernel, name='grads', out_shape=[sds((EL, D, W), F32...  11.6 us
    ppermute x1, starting transfers between devices, step(): across = lax.ppermute(dxh, 'etp', [(0, 3), (3, 0)])  3.66 us
  transfers between devices with their start and end apart: 3, of which 0 were waited for; matrix products, arithmetic and copies ran while one was open for 0% of the time, Pallas kernels for 14%

profile of v4, /device:TPU:0, one launch (start us, length us, event | category | flops | bytes accessed | tf_op | source)
XLA Modules:
  0.0 85.6 jit_solution(12968842459487208100)
XLA Ops:
  0.6 66.2 %line.1 = (bf16[128,1536]{1,0:T(8,128)(2,1)}, bf16[128,768]{1,0:T(8,128)(2,1)}, bf16[160,1536]{1,0:T(8,128)(2,1)}, bf16[160,1536]{1,0:T(8,128)(2,1)}, bf16[3,160...) custom-call(bf16[128,1536]{1,0:T(8,128)(2,1)} %x_h.1, ...), custom_call_target="tpu_custom_call" | custom-call | tf_op jit(solution)/shard_map/line/pallas_call | solution.py:739
  66.8 1.3 %collective-permute-start = (bf16[128,768]{1,0:T(8,128)(2,1)}, bf16[128,768]{1,0:T(8,128)(2,1)S(1)}, u32[]{:S(2)}, u32[]{:S(2)}) collective-permute-start(bf16[128,768]{1,0:T(8,128)(2,1)} %get-tuple-element.33), channel_id=1, source_target_pairs={{0,4},{12,8},{1,5},{13,9},{2,6},{14,10},{3,7},{15,11},{16,20},{28,... | collective-permute-start | bytes 589832 | tf_op jit(solution)/shard_map/ppermute | solution.py:751
  68.1 1.3 %collective-permute-start.1 = (bf16[128,768]{1,0:T(8,128)(2,1)}, bf16[128,768]{1,0:T(8,128)(2,1)S(1)}, u32[]{:S(2)}, u32[]{:S(2)}) collective-permute-start(bf16[128,768]{1,0:T(8,128)(2,1)} %get-tuple-element.33), channel_id=1, source_target_pairs={{0,8},{12,4},{1,9},{13,5},{2,10},{14,6},{3,11},{15,7},{16,24},{28,... | collective-permute-start | bytes 589832 | tf_op jit(solution)/shard_map/ppermute | solution.py:750
  69.4 3.7 %collective-permute-start.2 = (bf16[128,768]{1,0:T(8,128)(2,1)}, bf16[128,768]{1,0:T(8,128)(2,1)S(1)}, u32[]{:S(2)}, u32[]{:S(2)}) collective-permute-start(bf16[128,768]{1,0:T(8,128)(2,1)} %get-tuple-element.33), channel_id=1, source_target_pairs={{0,12},{12,0},{1,13},{13,1},{2,14},{14,2},{3,15},{15,3},{16,28},{2... | collective-permute-start | bytes 589832 | tf_op jit(solution)/shard_map/ppermute | solution.py:749
  73.1 0.0 copy-start
  73.1 11.6 %grads.1 = (f32[10,1536,128]{2,1,0:T(8,128)}, f32[10,1536,128]{2,1,0:T(8,128)}, f32[10,128,1536]{2,1,0:T(8,128)}, f32[1536,128]{1,0:T(8,128)}, f32[1536,128]{1,0...) custom-call(bf16[160,1536]{1,0:T(8,128)(2,1)} %get-tuple-element.25.nr_h, ...), custom_call_target="tpu_custom_call" | custom-call | flops 30000001024 | bytes 32000000 | tf_op jit(solution)/shard_map/grads/pallas_call | solution.py:752
  84.8 0.0 collective-permute-done
  84.8 0.0 collective-permute-done.1
  84.8 0.0 collective-permute-done.2
  84.8 0.0 copy-done
  84.8 0.8 pad_maximum_fusion
  (1 shorter events, 0.0 us)
Async XLA Ops:
  66.8 17.9 %collective-permute-start = (bf16[128,768]{1,0:T(8,128)(2,1)}, bf16[128,768]{1,0:T(8,128)(2,1)S(1)}, u32[]{:S(2)}, u32[]{:S(2)}) collective-permute-start(bf16[128,768]{1,0:T(8,128)(2,1)} %get-tuple-element.33), channel_id=1, source_target_pairs={{0,4},{12,8},{1,5},{13,9},{2,6},{14,10},{3,7},{15,11},{16,20},{28,... | collective-permute-start | bytes 589832 | tf_op jit(solution)/shard_map/ppermute | solution.py:751
  68.1 16.6 %collective-permute-start.1 = (bf16[128,768]{1,0:T(8,128)(2,1)}, bf16[128,768]{1,0:T(8,128)(2,1)S(1)}, u32[]{:S(2)}, u32[]{:S(2)}) collective-permute-start(bf16[128,768]{1,0:T(8,128)(2,1)} %get-tuple-element.33), channel_id=1, source_target_pairs={{0,8},{12,4},{1,9},{13,5},{2,10},{14,6},{3,11},{15,7},{16,24},{28,... | collective-permute-start | bytes 589832 | tf_op jit(solution)/shard_map/ppermute | solution.py:750
  69.4 15.4 %collective-permute-start.2 = (bf16[128,768]{1,0:T(8,128)(2,1)}, bf16[128,768]{1,0:T(8,128)(2,1)S(1)}, u32[]{:S(2)}, u32[]{:S(2)}) collective-permute-start(bf16[128,768]{1,0:T(8,128)(2,1)} %get-tuple-element.33), channel_id=1, source_target_pairs={{0,12},{12,0},{1,13},{13,1},{2,14},{14,2},{3,15},{15,3},{16,28},{2... | collective-permute-start | bytes 589832 | tf_op jit(solution)/shard_map/ppermute | solution.py:749
  73.1 11.7 %copy-start = (bf16[128,768]{1,0:T(8,128)(2,1)S(1)}, bf16[128,768]{1,0:T(8,128)(2,1)}, u32[]{:S(2)}) copy-start(bf16[128,768]{1,0:T(8,128)(2,1)} %get-tuple-element.33) | copy-start | bytes 589828
